TPU v7x, 32 devices: a whole 2x2x4 slice. The times are simulated.
32 devices in a mesh: band: 4 (over z), sector: 8 (over y, x, core).
Axes of the slice: x: 2, y: 2, z: 4, core: 2. Of those that a mesh axis runs over, the one named last changes fastest.
Arguments:
- field: float32 [2, 640, 2, 2560], P(None, 'band', None, 'sector'), may hold values from -6 to 6
- depart: int32 [2, 640, 80], P(None, 'band', 'sector'), may hold values from -2 to 2
- interp_weight: bfloat16 [2, 640, 80, 64, 32], P(None, 'band', 'sector'), may hold values from -0.75 to 0.75
- legendre: float32 [640, 640, 1281], P('sector', 'band'), may hold values from -0.25 to 0.25
- damping: float32 [2], replicated, may hold values from 0.3 to 30
Outputs:
- new_field: float32 [2, 640, 2, 2560], P(None, 'band', None, 'sector')
All inputs are finite; a program needn't handle non-finite values.
Results may differ from a plain program's by a relative error of at most 0.0003.
Values sent between devices are 32-bit elements; how exact they have to be, the bound alone decides.
No kernel may reach another device: no remote copies, remote signals or barrier semaphores. Data moves between devices by JAX's collectives and lax.ppermute only.
A program may use at most 192 MiB of HBM per device.

v0:
```python
import math

import jax
import jax.numpy as jnp
from jax import lax
from jax.sharding import PartitionSpec as P

HIGHEST = lax.Precision.HIGHEST


def padded(x, sides, width):
    for axis, dim in sides:
        peers, length = (lax.axis_size(axis), x.shape[dim])
        up = [(i, (i + 1) % peers) for i in range(peers)]
        down = [(j, i) for i, j in up]
        last = lax.slice_in_dim(x, length - width, length, axis=dim)
        leading = lax.slice_in_dim(x, 0, width, axis=dim)
        before = lax.ppermute(last, axis, up)
        after = lax.ppermute(leading, axis, down)
        x = jnp.concatenate([before, x, after], axis=dim)
    return x


def phase(product, lon_count):
    return 2.0 * math.pi / lon_count * (product % lon_count).astype(jnp.float32)


def forward_table(lon_count, m_count, pair_total):
    longitude = jnp.arange(lon_count, dtype=jnp.int32)[:, None]
    pair_range = jnp.arange(pair_total, dtype=jnp.int32)[None, :]
    lower_angle = phase(longitude * pair_range, lon_count)
    upper_angle = phase(longitude * (m_count - 1 - pair_range), lon_count)
    table = jnp.stack(
        [jnp.cos(lower_angle), -jnp.sin(lower_angle), jnp.cos(upper_angle), -jnp.sin(upper_angle)],
        axis=1,
    )
    return table / lon_count


def inverse_table(lon_count, m_count, pair_total):
    pair_range = jnp.arange(pair_total, dtype=jnp.int32)[:, None]
    longitude = jnp.arange(lon_count, dtype=jnp.int32)[None, :]
    lower_angle = phase(pair_range * longitude, lon_count)
    upper_angle = phase((m_count - 1 - pair_range) * longitude, lon_count)
    lower_scale = jnp.where(pair_range == 0, 1.0, 2.0)
    return jnp.stack(
        [
            lower_scale * jnp.cos(lower_angle),
            -lower_scale * jnp.sin(lower_angle),
            2.0 * jnp.cos(upper_angle),
            -2.0 * jnp.sin(upper_angle),
        ],
        axis=0,
    )


def pair_masks(pair_index, m_count, row_count):
    column = jnp.arange(row_count, dtype=jnp.int32)[None, :]
    limit = (m_count - pair_index)[:, None]
    leading = column < limit
    lag_value = jnp.where(leading, column, column - limit)
    odd_rows = lag_value % 2 == 1
    degree = jnp.where(leading, pair_index[:, None] + column, column - 1)
    return (leading, odd_rows, degree)


def analyse(wave, legendre, leading, odd_rows):
    stacked = jnp.stack([wave[0] + wave[1], wave[0] - wave[1]])
    product = jnp.einsum("svcpl,plk->svcpk", stacked, legendre, precision=HIGHEST)
    chosen = jnp.where(odd_rows, product[1], product[0])
    return jnp.where(leading, chosen[:, 0:2], chosen[:, 2:4])


def solve_modes(spectrum, damping_levels, degree, m_count):
    ratio = (degree * (degree + 1)).astype(jnp.float32) / float(m_count * m_count)
    return spectrum / (1.0 + damping_levels[:, None, None, None] * ratio[None, None])


def synthesise(spectrum, legendre, leading, odd_rows):
    lower = jnp.where(leading, spectrum, 0.0)
    upper = jnp.where(leading, 0.0, spectrum)
    northern = jnp.concatenate([lower, upper], axis=1)
    southern = jnp.where(odd_rows, -northern, northern)
    stacked = jnp.stack([northern, southern])
    return jnp.einsum("hvcpk,plk->hvcpl", stacked, legendre, precision=HIGHEST)


def advect(field, depart, interp_weight):
    tile_width = interp_weight.shape[-1]
    tile_count = depart.shape[2]
    extended = padded(field, (("sector", 3),), 3 * tile_width)
    pieces = extended.reshape(
        field.shape[0], field.shape[1], field.shape[2], tile_count + 6, tile_width
    )
    window = jnp.zeros(field.shape[:3] + (tile_count, 2 * tile_width), jnp.float32)
    for offset in range(-2, 3):
        lead_part = pieces[:, :, :, 3 + offset : 3 + offset + tile_count]
        next_part = pieces[:, :, :, 4 + offset : 4 + offset + tile_count]
        candidate = jnp.concatenate([lead_part, next_part], axis=4)
        window = jnp.where((depart == offset)[:, :, None, :, None], candidate, window)
    result = jnp.einsum(
        "hlvtj,hltji->hlvti", window, interp_weight.astype(jnp.float32), precision=HIGHEST
    )
    return result.reshape(field.shape)


def local(field, depart, interp_weight, legendre, damping):
    advected = advect(field, depart, interp_weight)
    columns = lax.all_to_all(advected, "sector", split_axis=1, concat_axis=3, tiled=True)
    lon_count = columns.shape[3]
    row_count = legendre.shape[2]
    m_count = row_count - 1
    pair_total = m_count // 2
    fourier = jnp.einsum(
        "hlvn,ncp->hvcpl", columns, forward_table(lon_count, m_count, pair_total), precision=HIGHEST
    )
    wave = lax.all_to_all(fourier, "sector", split_axis=3, concat_axis=4, tiled=True)
    pair_local = legendre.shape[0]
    pair_index = lax.axis_index("sector") * pair_local + jnp.arange(pair_local, dtype=jnp.int32)
    leading, odd_rows, degree = pair_masks(pair_index, m_count, row_count)
    partial_value = analyse(wave, legendre, leading, odd_rows)
    summed = lax.psum(partial_value, "band")
    spectrum = solve_modes(summed, damping, degree, m_count)
    synthesis = synthesise(spectrum, legendre, leading, odd_rows)
    returned = lax.all_to_all(synthesis, "sector", split_axis=4, concat_axis=3, tiled=True)
    gridded = jnp.einsum(
        "hvcpl,cpn->hlvn",
        returned,
        inverse_table(lon_count, m_count, pair_total),
        precision=HIGHEST,
    )
    return lax.all_to_all(gridded, "sector", split_axis=3, concat_axis=1, tiled=True)


def solution(mesh):
    return jax.shard_map(
        local,
        mesh=mesh,
        in_specs=(
            P(None, "band", None, "sector"),
            P(None, "band", "sector"),
            P(None, "band", "sector", None, None),
            P("sector", "band", None),
            P(),
        ),
        out_specs=P(None, "band", None, "sector"),
        check_vma=False,
    )
```

profile of v0, /device:TPU:0, one launch (start us, length us, event | category | flops | bytes accessed | tf_op | source)
XLA Modules:
  0.0 574.6 jit_solution(14221418994076441532)
XLA Ops:
  11.6 28.4 %fusion.32 = (f32[2560,1,640]{2,0,1:T(8,128)}, f32[2560,1,640]{2,0,1:T(8,128)}) fusion(s32[640]{0:T(1024)S(1)} %iota_subtract_fusion), kind=kLoop, calls=%fused_computation.40 | loop fusion | flops 16384000 | bytes 13109760 | tf_op jit(solution)/shard_map/cos | solution.py:34
  40.2 47.9 %copy.114 = bf16[2,160,10,64,32]{3,4,2,1,0:T(8,128)(2,1)} copy(bf16[2,160,10,64,32]{1,4,3,2,0:T(8,128)(2,1)} %param.7) | data formatting | bytes 26214400 | tf_op args[2]
  94.7 43.8 %convolution_bitcast_fusion = f32[2,160,2,10,32]{4,2,3,1,0:T(2,128)S(1)} fusion(f32[2,160,2,10,64]{4,2,3,1,0:T(2,128)} %copy.113, bf16[2,160,10,64,32]{3,4,2,1,0:T(8,128)(2,1)} %copy.114), kind=kOutput, calls=%fused_computation.67 | convolution fusion | flops 157286400 | bytes 15564800 | tf_op jit(solution)/shard_map/hlvtj,hltji->hlvti/dot_general | solution.py:101
  148.2 27.9 %sine_negate_fusion.1 = (f32[2560,1,640]{2,0,1:T(8,128)}, f32[2560,1,640]{2,0,1:T(8,128)}) fusion(), kind=kLoop, calls=%fused_computation.41 | loop fusion | flops 16384000 | bytes 13107200 | tf_op jit(solution)/shard_map/neg | solution.py:34
  176.7 19.3 %fusion.54 = f32[2,2,4,640,20]{3,4,1,0,2:T(8,128)S(1)} fusion(f32[2,20,2,2560,1]{3,1,2,0,4:T(8,128)S(1)} %reshape.528, f32[2560,1,640]{2,0,1:T(8,128)} %get-tuple-element.25, f32[2560,1,640]{2,0,1:T(8,128)} %get-tuple-element.24, f32[2560,1,640]{2,0,1:T(8,128)} %get-tuple-element.30, f32[2560,1,640]{2,0,1:T(8,128)} %get-tuple-element.31), kind=kOutput, calls=%fused_computation.78 | convolution fusion | flops 6317670400 | bytes 27852800 | tf_op jit(solution)/shard_map/hlvn,ncp->hvcpl/dot_general | solution.py:114
  196.0 5.0 copy.120
  201.0 10.6 %reshape.535 = f32[8,1,25600]{2,1,0:T(1,128)} reshape(f32[640,4,2,2,20]{4,3,2,1,0:T(2,128)} %bitcast.90) | data formatting | bytes 1638400
  211.6 4.2 all-to-all-start.1
  217.1 11.6 %all-to-all-done.1 = f32[8,1,25600]{2,1,0:T(1,128)S(1)} async-done(((f32[8,1,25600]{2,1,0:T(1,128)}), f32[8,1,25600]{2,1,0:T(1,128)S(1)}, u32[]{:S(2)}, u32[]{:S(2)}) %all-to-all-start.1) | async-done | bytes 819232 | tf_op jit(solution)/shard_map/all_to_all | solution.py:117
  231.8 10.9 %reshape.536 = f32[640,4,2,2,20]{4,3,2,1,0:T(2,128)} reshape(f32[8,25600]{1,0:T(8,128)S(1)} %reduce) | data formatting | bytes 1638400
  242.7 6.0 %copy.141 = f32[2,2,4,8,80,20]{4,3,2,5,1,0:T(8,128)S(1)} copy(f32[2,2,4,8,80,20]{5,1,0,2,4,3:T(2,128)} %bitcast.91) | data formatting | bytes 1638400 | tf_op jit(solution)/shard_map/all_to_all | solution.py:117
  250.4 42.7 %fusion.44 = f32[2,2,4,80,1281]{4,2,1,0,3:T(4,128)} fusion(f32[80,160,1281]{2,1,0:T(8,128)} %param.8, f32[2,2,4,80,160]{4,2,1,0,3:T(4,128)S(1)} %fusion.83), kind=kOutput, calls=%fused_computation.61 | convolution fusion | flops 3148185600 | bytes 72965120 | tf_op jit(solution)/shard_map/svcpl,plk->svcpk/dot_general | solution.py:69
  293.2 4.5 fusion.48
  300.8 28.3 %sine_multiply_fusion.1 = (f32[1,640,2560]{2,1,0:T(8,128)}, f32[1,640,2560]{2,1,0:T(8,128)}) fusion(f32[640]{0:T(1024)S(1)} %fusion.65, f32[640]{0:T(1024)S(1)} %fusion.64), kind=kLoop, calls=%fused_computation.51 | loop fusion | flops 18022400 | bytes 13112320 | tf_op jit(solution)/shard_map/mul | solution.py:49
  329.0 48.0 %all-reduce.2.cloned.1.call-done = f32[2,2,80,1281]{3,1,0,2:T(2,128)} async-done(((f32[2,2,80,1281]{3,1,0,2:T(2,128)}), f32[2,2,80,1281]{3,1,0,2:T(2,128)}) %all-reduce.2.cloned.1.call-update) | async-done | bytes 1639696 | tf_op jit(solution)/shard_map/psum | solution.py:122
  386.5 73.3 %fusion.49 = f32[2,2,4,80,160]{4,2,1,0,3:T(4,128)S(1)} fusion(f32[80,160,1281]{2,1,0:T(8,128)} %param.8, f32[1,2,4,80,1281]{4,2,1,3,0:T(4,128)S(1)} %negate_select_fusion, f32[1,2,4,80,1281]{4,2,1,3,0:T(4,128)S(1)} %maximum_bitcast_fusion.4), kind=kOutput, calls=%fused_computation.77 | convolution fusion | flops 3149825280 | bytes 72965120 | tf_op jit(solution)/shard_map/hvcpk,plk->hvcpl/dot_general | solution.py:85
  461.4 4.1 all-to-all-start.2
  465.6 29.7 %cosine_multiply_fusion = (f32[1,640,2560]{2,1,0:T(8,128)}, f32[1,640,2560]{2,1,0:T(8,128)}) fusion(s32[640]{0:T(1024)S(1)} %iota_subtract_fusion), kind=kLoop, calls=%fused_computation.47 | loop fusion | flops 18022400 | bytes 13109760 | tf_op jit(solution)/shard_map/mul | solution.py:50
  496.5 19.2 %fusion.47 = f32[2,20,2,2560]{3,1,2,0:T(8,128)S(1)} fusion(f32[2,2,4,640,20]{3,4,2,1,0:T(8,128)S(1)} %reshape.534, f32[1,640,2560]{2,1,0:T(8,128)} %get-tuple-element.23, f32[1,640,2560]{2,1,0:T(8,128)} %get-tuple-element.22, f32[1,640,2560]{2,1,0:T(8,128)} %get-tuple-element.32, f32[1,640,2560]{2,1,0:T(8,128)} %get-tuple-element.33), kind=kOutput, calls=%fused_computation.62 | convolution fusion | flops 6311116800 | bytes 27852800 | tf_op jit(solution)/shard_map/hvcpl,cpn->hlvn/dot_general | solution.py:126
  515.7 5.0 copy.132
  520.7 9.9 %reshape.537 = f32[8,1,25600]{2,1,0:T(1,128)S(1)} reshape(f32[2560,2,2,20]{3,2,1,0:T(2,128)} %bitcast.92) | data formatting | bytes 1638400
  530.6 17.1 %all_to_all.69 = f32[8,1,25600]{2,1,0:T(1,128)S(1)} all-to-all(f32[8,1,25600]{2,1,0:T(1,128)S(1)} %reshape.537), channel_id=1, replica_groups=mesh['band'=4,'sector'=8] {'sector'}, dimensions={0} | all-to-all | bytes 1638400 | tf_op jit(solution)/shard_map/all_to_all | solution.py:132
  550.3 10.9 %reshape.538 = f32[2560,2,2,20]{3,2,1,0:T(2,128)} reshape(f32[8,25600]{1,0:T(8,128)S(1)} %reduce.1) | data formatting | bytes 1638400
  561.1 5.0 copy.144
  (58 shorter events, 47.7 us)
Async XLA Ops:
  8.2 79.9 %collective-permute-start = (f32[2,160,2,96]{1,3,2,0:T(8,128)S(1)}, f32[2,160,2,96]{1,3,2,0:T(8,128)S(1)}, u32[]{:S(2)}, u32[]{:S(2)}) collective-permute-start(f32[2,160,2,96]{1,3,2,0:T(8,128)S(1)} %get-tuple-element.15), channel_id=1, source_target_pairs={{0,1},{1,2},{2,3},{3,4},{4,5},{5,6},{6,7},{7,0},{8,9},{9,10},{10,1... | collective-permute-start | bytes 737288 | tf_op jit(solution)/shard_map/ppermute | solution.py:18
  8.7 79.4 %collective-permute-start.1 = (f32[2,160,2,96]{1,3,2,0:T(8,128)S(1)}, f32[2,160,2,96]{1,3,2,0:T(8,128)S(1)}, u32[]{:S(2)}, u32[]{:S(2)}) collective-permute-start(f32[2,160,2,96]{1,3,2,0:T(8,128)S(1)} %get-tuple-element.16), channel_id=1, source_target_pairs={{1,0},{2,1},{3,2},{4,3},{5,4},{6,5},{7,6},{0,7},{9,8},{10,9},{11,1... | collective-permute-start | bytes 737288 | tf_op jit(solution)/shard_map/ppermute | solution.py:19
  11.6 28.4 %copy-start.1 = (s32[2,160,10]{1,0,2:T(2,128)S(1)}, s32[2,160,10]{1,0,2:T(2,128)}, u32[]{:S(2)}) copy-start(s32[2,160,10]{1,0,2:T(2,128)} %param.6) | copy-start | bytes 38404
  144.2 31.9 %all-to-all-start = ((f32[2,160,2,320]{3,2,0,1:T(2,128)}), f32[2,160,2,320]{3,2,0,1:T(2,128)S(1)}, u32[]{:S(2)}, u32[]{:S(2)}) async-start(f32[2,160,2,320]{3,2,0,1:T(2,128)} %copy.116), calls=%async_computation | async-start | bytes 1966080 | tf_op jit(solution)/shard_map/all_to_all | solution.py:109
  211.6 17.1 %all-to-all-start.1 = ((f32[8,1,25600]{2,1,0:T(1,128)}), f32[8,1,25600]{2,1,0:T(1,128)S(1)}, u32[]{:S(2)}, u32[]{:S(2)}) async-start(f32[8,1,25600]{2,1,0:T(1,128)} %reshape.535), calls=%async_computation.1 | async-start | bytes 1638400 | tf_op jit(solution)/shard_map/all_to_all | solution.py:117
  215.8 161.2 %all-reduce.2.cloned.1.call-start = ((), (), s32[]{:S(2)}) async-start(), calls=%async_computation.4 | async-start | bytes 3604480 | tf_op jit(solution)/shard_map/psum | solution.py:122
  250.4 42.8 %copy-start = (pred[80,1281]{1,0:T(8,128)(4,1)S(1)}, pred[80,1281]{1,0:T(8,128)(4,1)}, u32[]{:S(2)}) copy-start(pred[80,1281]{1,0:T(8,128)(4,1)} %get-tuple-element.26) | copy-start | bytes 307444
  297.6 2.7 copy-start.2
  461.4 33.8 %all-to-all-start.2 = ((f32[2,2,4,80,160]{3,2,1,0,4:T(4,128)}), f32[2,2,4,80,160]{3,2,1,0,4:T(4,128)S(1)}, u32[]{:S(2)}, u32[]{:S(2)}) async-start(f32[2,2,4,80,160]{3,2,1,0,4:T(4,128)} %copy.128), calls=%async_computation.2 | async-start | bytes 2621440 | tf_op jit(solution)/shard_map/all_to_all | solution.py:125
Sparse Core Ops, SparseCore 0:
  300.4 76.5 all-reduce.1
where the time goes:
time: 584 us; the launch traced here: 575 us
  matrix products  198 us (34%)
  other arithmetic  140 us (24%)
  local copies, waits for them, and re-layouts  130 us (22%)
  waiting for transfers between devices  59.6 us (10%)
  blocking collectives  17.1 us (3%)
  starting transfers between devices  15.9 us (3%)
  between operations  13.9 us (2%)
    unnamed x12, local copies, waits for them, and re-layouts  91.7 us
    dot_general x1, matrix products, synthesise(): return jnp.einsum('hvcpk,plk->hvcpl', stacked, legendre, precision=HIGHEST)  73.3 us
    psum x1, waiting for transfers between devices, local(): summed = lax.psum(partial_value, 'band')  48 us
    dot_general x1, matrix products, advect(): jnp.einsum('hlvtj,hltji->hlvti', window, interp_weight.astype(jnp.float32...  43.8 us
    dot_general x1, matrix products, analyse(): jnp.einsum('svcpl,plk->svcpk', stacked, legendre, precision=HIGHEST)  42.7 us
    mul x1, other arithmetic, inverse_table(): 2.0 * jnp.cos(upper_angle)  29.7 us
    cos x1, other arithmetic, forward_table(): jnp.cos(upper_angle)  28.4 us
    mul x1, other arithmetic, inverse_table(): -lower_scale * jnp.sin(lower_angle)  28.3 us
  transfers between devices with their start and end apart: 6, of which 2 were waited for; matrix products, arithmetic and copies ran while one was open for 29% of the time, Pallas kernels for 0%

commit v1 on v0

v1 whole, which is shorter than its diff:
```python
import functools
import math

import jax
import jax.numpy as jnp
import numpy as np
from jax import lax
from jax.experimental import pallas as pl
from jax.experimental.pallas import tpu as pltpu
from jax.sharding import PartitionSpec as P

REACH_BACK = 2
REACH_AHEAD = 3
CHUNKS = 2
LANES = 128
WIDE = 256
F32 = jnp.float32
BF16 = jnp.bfloat16


def params(*semantics):
    return pltpu.CompilerParams(dimension_semantics=semantics, vmem_limit_bytes=48 * 1024 * 1024)


def cost(flops, moved):
    return pl.CostEstimate(flops=int(flops), bytes_accessed=int(moved), transcendentals=0)


def split(x):
    high = x.astype(BF16)
    low = (x - high.astype(F32)).astype(BF16)
    return high, low


def split_np(x):
    high = np.asarray(x, np.float32).astype(jnp.bfloat16)
    low = (np.asarray(x, np.float64) - high.astype(np.float64)).astype(np.float32).astype(jnp.bfloat16)
    return high, low


def advect_kernel(field_ref, before_ref, after_ref, depart_ref, weight_ref, out_ref, extended, window, *, width, parts, share):
    tile = pl.program_id(1)
    levels, local = field_ref.shape[1], field_ref.shape[2]
    back, ahead = REACH_BACK * width, REACH_AHEAD * width

    @pl.when(tile == 0)
    def _():
        for v in range(levels):
            extended[v, 0:back] = before_ref[0, v]
            extended[v, back : back + local] = field_ref[0, v]
            extended[v, back + local : back + local + ahead] = after_ref[0, v]

    depart = depart_ref[0, 0]
    start = pl.multiple_of(tile * width, width)
    for v in range(levels):
        for half in range(0, 2 * width, 8):
            picked = None
            for step in range(2 * REACH_BACK + 1):
                rows = extended[v, pl.ds(start + step * width + half, 8), :]
                chosen = depart == (step - REACH_BACK)
                picked = rows if picked is None else jnp.where(chosen, rows, picked)
            window[v, half : half + 8] = picked
    columns = field_ref.shape[3]

    def body(block, totals):
        for j in range(8):
            row = block * 8 + j
            weight = weight_ref[0, 0, row].astype(F32)
            totals = tuple(
                totals[v] + window[v, pl.ds(row, 1), :] * weight for v in range(levels)
            )
        return totals

    zero = jnp.zeros((width, columns), F32)
    totals = lax.fori_loop(0, 2 * width // 8, body, (zero,) * levels)
    for v in range(levels):
        for part in range(parts):
            out_ref[v * parts + part, :, 0:share] = totals[v][:, part * share : (part + 1) * share]


def advect(field, depart, interp_weight, sectors):
    hemis, lats, levels, local = field.shape
    width = interp_weight.shape[-1]
    tiles = depart.shape[2]
    parts = sectors // (hemis * levels)
    share = lats // parts
    turned = jnp.transpose(field, (0, 2, 3, 1))
    up = [(i, (i + 1) % sectors) for i in range(sectors)]
    down = [(j, i) for i, j in up]
    before = lax.ppermute(turned[:, :, local - REACH_BACK * width :], "sector", up)
    after = lax.ppermute(turned[:, :, : REACH_AHEAD * width], "sector", down)
    weights = jnp.transpose(interp_weight, (0, 2, 3, 4, 1))
    offsets = jnp.transpose(depart, (0, 2, 1))[:, :, None, :]
    return pl.pallas_call(
        functools.partial(advect_kernel, width=width, parts=parts, share=share),
        grid=(hemis, tiles),
        in_specs=[
            pl.BlockSpec((1, levels, local, lats), lambda h, t: (h, 0, 0, 0)),
            pl.BlockSpec((1, levels, REACH_BACK * width, lats), lambda h, t: (h, 0, 0, 0)),
            pl.BlockSpec((1, levels, REACH_AHEAD * width, lats), lambda h, t: (h, 0, 0, 0)),
            pl.BlockSpec((1, 1, 1, lats), lambda h, t: (h, t, 0, 0)),
            pl.BlockSpec((1, 1, 2 * width, width, lats), lambda h, t: (h, t, 0, 0, 0)),
        ],
        out_specs=pl.BlockSpec((levels * parts, width, LANES), lambda h, t: (h, t, 0)),
        out_shape=jax.ShapeDtypeStruct((sectors, local, LANES), F32),
        scratch_shapes=[
            pltpu.VMEM((levels, local + (REACH_BACK + REACH_AHEAD) * width, lats), F32),
            pltpu.VMEM((levels, 2 * width, lats), F32),
        ],
        compiler_params=params("arbitrary", "arbitrary"),
        cost_estimate=cost(4 * hemis * tiles * levels * 2 * width * width * lats * 4, interp_weight.size * 3),
        name="advect",
    )(turned, before, after, offsets, weights)


def fourier_tables(lon_count, radix):
    inner = lon_count // radix
    waves = lon_count // 2
    slots = waves // 2 // radix
    index = np.arange(slots)
    direct = index
    mirror = waves // radix - 1 - index
    rows = []
    for kind in range(2):
        for component in range(4):
            degree = direct if component < 2 else mirror
            source = degree if kind == 0 else inner - 1 - degree
            angle = 2.0 * np.pi * ((source[:, None] * np.arange(inner)[None, :]) % inner) / inner
            if component % 2 == 0:
                row = np.concatenate([np.cos(angle), np.sin(angle)], axis=1)
            else:
                sign = 1.0 if kind == 0 else -1.0
                row = sign * np.concatenate([-np.sin(angle), np.cos(angle)], axis=1)
            rows.append(row)
    matrix = np.concatenate(rows, axis=0)
    order = np.arange(radix // 2 + 1)[:, None] * np.arange(inner)[None, :]
    angle = 2.0 * np.pi * (order % lon_count) / lon_count
    twiddle = np.stack([np.cos(angle), -np.sin(angle)], axis=1).astype(np.float32)
    return matrix, twiddle


def scaled(x, factor):
    if abs(factor - 1.0) < 1e-12:
        return x
    if abs(factor + 1.0) < 1e-12:
        return -x
    return x * np.float32(factor)


def combine(terms):
    total = None
    for factor, x in terms:
        if abs(factor) < 1e-12:
            continue
        total = scaled(x, factor) if total is None else total + scaled(x, factor)
    return total


def products(high_ref, low_ref, rows, depth, x):
    x_high, x_low = split(x)
    both = jnp.concatenate([x_high, x_low], axis=1)
    first = jnp.dot(high_ref[0:rows, 0:depth], both, preferred_element_type=F32)
    second = jnp.dot(low_ref[0:rows, 0:depth], x_high, preferred_element_type=F32)
    return first[:, 0:LANES] + first[:, LANES:] + second


def places(a, radix):
    residues = [a] if a in (0, radix // 2) else [a, radix - a]
    result = []
    for residue in residues:
        for component in range(4):
            first = residue if component < 2 else radix - 1 - residue
            result.append(first * 4 + component)
    return result


def forward_kernel(x_ref, high_ref, low_ref, twiddle_ref, out_ref, *, radix):
    inner = x_ref.shape[0] // radix
    slots = out_ref.shape[0] // (4 * radix)
    x = [x_ref[s * inner : (s + 1) * inner] for s in range(radix)]
    middle = radix // 2
    even = {s: x[s] + x[radix - s] for s in range(1, middle)}
    odd = {s: x[s] - x[radix - s] for s in range(1, middle)}
    for a in range(middle + 1):
        angle = [2.0 * math.pi * ((a * s) % radix) / radix for s in range(radix)]
        real = combine([(1.0, x[0]), (math.cos(angle[middle]), x[middle])] + [(math.cos(angle[s]), even[s]) for s in even])
        imag = combine([(-math.sin(angle[s]), odd[s]) for s in odd])
        where = places(a, radix)
        if a == 0:
            result = products(high_ref, low_ref, len(where) * slots, inner, real)
        else:
            cos, sin = twiddle_ref[a, 0], twiddle_ref[a, 1]
            turned_real = cos * real if imag is None else cos * real - sin * imag
            turned_imag = sin * real if imag is None else sin * real + cos * imag
            turned = jnp.concatenate([turned_real, turned_imag], axis=0)
            result = products(high_ref, low_ref, len(where) * slots, 2 * inner, turned)
        for n, first in enumerate(where):
            out_ref[pl.ds(first, slots, stride=4 * radix), :] = result[n * slots : (n + 1) * slots]


def inverse_kernel(z_ref, high_ref, low_ref, twiddle_ref, out_ref, *, radix):
    inner = out_ref.shape[0] // radix
    slots = z_ref.shape[0] // (4 * radix)
    middle = radix // 2
    reals, imags = [], []
    for a in range(middle + 1):
        where = places(a, radix)
        pieces = [z_ref[pl.ds(first, slots, stride=4 * radix), :] for first in where]
        if a == 0:
            row = lax.broadcasted_iota(jnp.int32, pieces[0].shape, 0)
            pieces[0] = jnp.where(row == 0, 0.5 * pieces[0], pieces[0])
        column = jnp.concatenate(pieces, axis=0)
        depth = len(where) * slots
        if a == 0:
            reals.append(products(high_ref, low_ref, inner, depth, column))
            imags.append(None)
            continue
        result = products(high_ref, low_ref, 2 * inner, depth, column)
        real, imag = result[0:inner], result[inner:]
        cos, sin = twiddle_ref[a, 0], twiddle_ref[a, 1]
        reals.append(cos * real + sin * imag)
        imags.append(None if a == middle else cos * imag - sin * real)
    for s in range(middle + 1):
        angle = [2.0 * math.pi * ((a * s) % radix) / radix for a in range(middle + 1)]
        even = combine([(math.cos(angle[a]), reals[a]) for a in range(middle + 1)])
        odd = combine([(-math.sin(angle[a]), imags[a]) for a in range(1, middle)])
        if s == 0 or s == middle:
            out_ref[s * inner : (s + 1) * inner] = even
        else:
            out_ref[s * inner : (s + 1) * inner] = even + odd
            other = radix - s
            out_ref[other * inner : (other + 1) * inner] = even - odd


def transform(kernel, x, high, low, twiddle, radix, name):
    rows = x.shape[0]
    return pl.pallas_call(
        functools.partial(kernel, radix=radix),
        out_shape=jax.ShapeDtypeStruct((rows, LANES), F32),
        compiler_params=pltpu.CompilerParams(vmem_limit_bytes=48 * 1024 * 1024),
        cost_estimate=cost(3 * 2 * high.size * LANES * radix, 4 * rows * LANES * 4),
        name=name,
    )(x, high, low, twiddle)


def row_masks(pair, waves, shape, first):
    column = first + lax.broadcasted_iota(jnp.int32, shape, 1)
    limit = waves - pair
    leading = column < limit
    lag = jnp.where(leading, column, column - limit)
    odd = (lag & 1) == 1
    return column, leading, odd


def ranges(count):
    edges = list(range(0, count - count % WIDE, WIDE)) + [count]
    return list(zip(edges[:-1], edges[1:]))


def gather_lats(z_ref, hemi, level, levels, parts, share, start):
    rows = [z_ref[(hemi * levels + level) * parts + part, pl.ds(start, 8), 0:share] for part in range(parts)]
    return jnp.concatenate(rows, axis=1)


def analyse_kernel(place_ref, z_ref, legendre_ref, out_ref, *, levels, parts, share):
    step = place_ref[0] + pl.program_id(0)
    count = legendre_ref.shape[2]
    waves = count - 1
    start = pl.multiple_of(step * 8, 8)
    sums, differences = [], []
    for v in range(levels):
        north = gather_lats(z_ref, 0, v, levels, parts, share, start)
        south = gather_lats(z_ref, 1, v, levels, parts, share, start)
        sums.append(north + south)
        differences.append(north - south)
    stacks = []
    for which in range(2):
        low, high = which * 4, which * 4 + 4
        wave = jnp.concatenate([x[low:high] for x in sums + differences], axis=0)
        wave_high, wave_low = split(wave)
        stacks.append((jnp.concatenate([wave_high, wave_low], axis=0), wave_high))
    for first, last in ranges(count):
        picked = []
        for which in range(2):
            both, wave_high = stacks[which]
            rows = both.shape[0] // 2
            high, low = split(legendre_ref[which, :, first:last])
            product = jnp.dot(both, high, preferred_element_type=F32)
            product = product[0:rows] + product[rows:] + jnp.dot(wave_high, low, preferred_element_type=F32)
            pair = place_ref[1] + 2 * step + which
            shape = (rows // 2, last - first)
            _, leading, odd = row_masks(pair, waves, shape, first)
            chosen = jnp.where(odd, product[rows // 2 :], product[0 : rows // 2])
            if which == 0:
                picked.append(jnp.where(leading, chosen, jnp.roll(chosen, -2, axis=0)))
            else:
                picked.append(jnp.where(leading, jnp.roll(chosen, 2, axis=0), chosen))
        component = lax.broadcasted_iota(jnp.int32, picked[0].shape, 0) % 4
        out_ref[0, :, first:last] = jnp.where(component < 2, picked[0], picked[1])


def analyse(place, z, legendre, steps, levels):
    pairs, lats, count = legendre.shape
    parts = z.shape[0] // (2 * levels)
    share = lats // parts
    return pl.pallas_call(
        functools.partial(analyse_kernel, levels=levels, parts=parts, share=share),
        grid_spec=pltpu.PrefetchScalarGridSpec(
            num_scalar_prefetch=1,
            grid=(steps,),
            in_specs=[
                pl.BlockSpec(z.shape, lambda i, place: (0, 0, 0)),
                pl.BlockSpec((2, lats, count), lambda i, place: (place[0] + i, 0, 0)),
            ],
            out_specs=pl.BlockSpec((1, 4 * levels, count), lambda i, place: (i, 0, 0)),
        ),
        out_shape=jax.ShapeDtypeStruct((steps, 4 * levels, count), F32),
        compiler_params=params("arbitrary"),
        cost_estimate=cost(16 * 2 * steps * lats * count * 20, 2 * steps * lats * count * 4),
        name="analyse",
    )(place, z, legendre)


def synthesise_kernel(place_ref, damping_ref, spectrum_ref, legendre_ref, *rest, levels, parts, share):
    out_ref = rest[-1]
    step = place_ref[0] + pl.program_id(0)
    count = legendre_ref.shape[2]
    waves = count - 1
    totals = [None, None]
    for first, last in ranges(count):
        spectrum = spectrum_ref[0, :, first:last]
        row = lax.broadcasted_iota(jnp.int32, spectrum.shape, 0)
        component = row % 4
        damping = jnp.full(spectrum.shape, damping_ref[levels - 1])
        for v in range(levels - 1):
            damping = jnp.where(row < 4 * (v + 1), damping_ref[v], damping) if v == 0 else damping
        for which in range(2):
            pair = place_ref[1] + 2 * step + which
            column, leading, odd = row_masks(pair, waves, spectrum.shape, first)
            degree = jnp.where(leading, pair + column, column - 1)
            ratio = (degree * (degree + 1)).astype(F32) / float(waves * waves)
            solved = spectrum / (1.0 + damping * ratio)
            if which == 0:
                doubled = jnp.where(component < 2, solved, jnp.roll(solved, 2, axis=0))
            else:
                doubled = jnp.where(component < 2, jnp.roll(solved, -2, axis=0), solved)
            keep = jnp.logical_xor(component >= 2, leading)
            north = jnp.where(keep, doubled, 0.0)
            south = jnp.where(odd, -north, north)
            high, low = split(jnp.concatenate([north, south], axis=0))
            both = jnp.concatenate([high, low], axis=0)
            legendre_high, legendre_low = split(legendre_ref[which, :, first:last])
            contract = (((1,), (1,)), ((), ()))
            one = lax.dot_general(legendre_high, both, contract, preferred_element_type=F32)
            two = lax.dot_general(legendre_low, both, contract, preferred_element_type=F32)
            total = one + two
            totals[which] = total if totals[which] is None else totals[which] + total
    rows = 4 * levels * 2
    waves_of = []
    for which in range(2):
        turned = jnp.transpose(totals[which], (1, 0))
        waves_of.append(turned[0:rows] + turned[rows:])
    for hemi in range(2):
        for v in range(levels):
            low = (hemi * levels + v) * 4
            block = jnp.concatenate([w[low : low + 4] for w in waves_of], axis=0)
            for part in range(parts):
                out_ref[(hemi * levels + v) * parts + part, :, 0:share] = block[:, part * share : (part + 1) * share]


def synthesise(place, damping, spectrum, legendre, previous, sectors):
    pairs, lats, count = legendre.shape
    levels = damping.shape[0]
    steps = spectrum.shape[0]
    parts = sectors // (2 * levels)
    share = lats // parts
    arguments = [place, damping, spectrum, legendre]
    in_specs = [
        pl.BlockSpec(memory_space=pltpu.SMEM),
        pl.BlockSpec((1, 4 * levels, count), lambda i, place: (i, 0, 0)),
        pl.BlockSpec((2, lats, count), lambda i, place: (place[0] + i, 0, 0)),
    ]
    aliases = {}
    if previous is not None:
        arguments.append(previous)
        in_specs.append(pl.BlockSpec(memory_space=pl.ANY))
        aliases = {4: 0}
    return pl.pallas_call(
        functools.partial(synthesise_kernel, levels=levels, parts=parts, share=share),
        grid_spec=pltpu.PrefetchScalarGridSpec(
            num_scalar_prefetch=1,
            grid=(steps,),
            in_specs=in_specs,
            out_specs=pl.BlockSpec((sectors, 8, LANES), lambda i, place: (0, place[0] + i, 0)),
        ),
        out_shape=jax.ShapeDtypeStruct((sectors, 4 * pairs, LANES), F32),
        input_output_aliases=aliases,
        compiler_params=params("arbitrary"),
        cost_estimate=cost(16 * 2 * steps * lats * count * 20, 2 * steps * lats * count * 4),
        name="synthesise",
    )(*arguments)


def solve(z, legendre, damping, sectors):
    pairs = legendre.shape[0]
    levels = damping.shape[0]
    bands = lax.axis_size("band")
    bit = lax.axis_index("band") % 2
    pair_start = lax.axis_index("sector") * pairs
    steps = pairs // (2 * 2 * CHUNKS)
    half = pairs // 4

    def place(side, chunk):
        return jnp.stack([side * half + chunk * steps, pair_start]).astype(jnp.int32)

    def swap(x, mask):
        return lax.ppermute(x, "band", [(i, i ^ mask) for i in range(bands)])

    def after(value, earlier):
        return value if earlier is None else lax.optimization_barrier((value, earlier))[0]

    masks = [1 << n for n in range(1, bands.bit_length()) if 1 << n < bands]
    sums, arrived, previous = [], [], None
    for c in range(CHUNKS):
        away = analyse(after(place(1 - bit, c), previous), z, legendre, steps, levels)
        kept = analyse(after(place(bit, c), away), z, legendre, steps, levels)
        previous = kept + swap(away, 1)
        sums.append(previous)
        arrived.append(swap(previous, masks[0]) if masks else jnp.zeros_like(previous))
    result = None
    for c in range(CHUNKS):
        total = sums[c] + after(arrived[c], sums[-1] if result is None else result)
        for mask in masks[1:]:
            total = total + swap(total, mask)
        other = swap(total, 1)
        result = synthesise(place(bit, c), damping, total, legendre, result, sectors)
        result = synthesise(place(1 - bit, c), damping, other, legendre, result, sectors)
    return result


def local(field, depart, interp_weight, legendre, damping):
    sectors = lax.axis_size("sector")
    hemis, lats, levels, local_lon = field.shape
    pairs = legendre.shape[0]
    lon_count = sectors * local_lon
    radix = math.gcd(sectors, pairs)
    matrix, twiddle = fourier_tables(lon_count, radix)
    forward_high, forward_low = split_np(matrix / lon_count)
    inverse_high, inverse_low = split_np(2.0 * matrix.T)
    twiddle = jnp.broadcast_to(jnp.asarray(twiddle)[..., None], twiddle.shape + (LANES,))

    def exchange(x, rows):
        return lax.all_to_all(x.reshape(sectors, rows, LANES), "sector", split_axis=0, concat_axis=0, tiled=True)

    advected = advect(field, depart, interp_weight, sectors)
    columns = exchange(advected, local_lon)
    fourier = transform(forward_kernel, columns.reshape(-1, LANES), forward_high, forward_low, twiddle, radix, "forward")
    z = exchange(fourier, 4 * pairs)
    synthesis = solve(z, legendre, damping, sectors)
    returned = exchange(synthesis, 4 * pairs)
    gridded = transform(inverse_kernel, returned.reshape(-1, LANES), inverse_high, inverse_low, twiddle, radix, "inverse")
    final = exchange(gridded, local_lon)
    parts = sectors // (hemis * levels)
    share = lats // parts
    final = final[:, :, :share].reshape(hemis, levels, parts, local_lon, share)
    return jnp.transpose(final, (0, 2, 4, 1, 3)).reshape(hemis, lats, levels, local_lon)


def solution(mesh):
    return jax.shard_map(
        local,
        mesh=mesh,
        in_specs=(
            P(None, "band", None, "sector"),
            P(None, "band", "sector"),
            P(None, "band", "sector", None, None),
            P("sector", "band", None),
            P(),
        ),
        out_specs=P(None, "band", None, "sector"),
        check_vma=False,
    )
```

time: 584 us -> 246 us (0.42); the launches traced: 575 us -> 244 us
  matrix products: 198 us -> 0 us
  other arithmetic: 140 us -> 0.45 us
  local copies, waits for them, and re-layouts: 130 us -> 4.46 us
  Pallas kernels: 0 us -> 124 us
  blocking collectives: 17.1 us -> 65.8 us
  waiting for transfers between devices: 59.6 us -> 31.2 us
  between operations: 13.9 us -> 0.23 us
    dot_general x5 -> x0, matrix products: 198 us -> none  [the longest x1 73.3 us: synthesise(): return jnp.einsum('hvcpk,plk->hvcpl', stacked, legendre, precision=HIGHEST)]
    pallas_call x0 -> x11, Pallas kernels: none -> 124 us  [the longest x4 53.5 us: synthesise(): pl.pallas_call(functools.partial(synthesise_kernel, levels=levels, parts=...]
    unnamed x12 -> x19, local copies, waits for them, and re-layouts: 91.7 us -> 2.51 us
    mul x2 -> x0, other arithmetic: 57.9 us -> none  [the longest x1 29.7 us: inverse_table(): 2.0 * jnp.cos(upper_angle)]
    all_to_all x1 -> x3, blocking collectives: 17.1 us -> 65.8 us  [exchange(): lax.all_to_all(x.reshape(sectors, rows, LANES), 'sector', split_axis=0, c...]
    psum x1 -> x0, waiting for transfers between devices: 48 us -> none  [local(): summed = lax.psum(partial_value, 'band')]
    cos x1 -> x0, other arithmetic: 28.4 us -> none  [forward_table(): jnp.cos(upper_angle)]
    neg x2 -> x0, other arithmetic: 27.9 us -> none  [the longest x1 27.9 us: forward_table(): -jnp.sin(lower_angle)]
  transfers between devices with their start and end apart: 6 -> 9, of which waited for: 2 -> 3; matrix products, arithmetic and copies ran while one was open for 29% -> 0% of each run, Pallas kernels for 0% -> 26%
where the time goes in v1:
time: 246 us; the launch traced here: 244 us
  Pallas kernels  124 us (50%)
  blocking collectives  65.8 us (27%)
  waiting for transfers between devices  31.2 us (13%)
  starting transfers between devices  18 us (7%)
  local copies, waits for them, and re-layouts  4.46 us (2%)
    all_to_all x3, blocking collectives, exchange(): lax.all_to_all(x.reshape(sectors, rows, LANES), 'sector', split_axis=0, c...  65.8 us
    pallas_call x4, Pallas kernels, synthesise(): pl.pallas_call(functools.partial(synthesise_kernel, levels=levels, parts=...  53.5 us
    pallas_call x4, Pallas kernels, analyse(): pl.pallas_call(functools.partial(analyse_kernel, levels=levels, parts=par...  45.5 us
    pallas_call x1, Pallas kernels, advect(): pl.pallas_call(functools.partial(advect_kernel, width=width, parts=parts,...  18.5 us
    all_to_all x1, waiting for transfers between devices, exchange(): lax.all_to_all(x.reshape(sectors, rows, LANES), 'sector', split_axis=0, c...  18 us
    ppermute x6, starting transfers between devices, swap(): return lax.ppermute(x, 'band', [(i, i ^ mask) for i in range(bands)])  10.9 us
    ppermute x1, waiting for transfers between devices, advect(): lax.ppermute(turned[:, :, local - REACH_BACK * width:], 'sector', up)  9 us
    pallas_call x2, Pallas kernels, transform(): pl.pallas_call(functools.partial(kernel, radix=radix), out_shape=jax.Shap...  6.44 us
  transfers between devices with their start and end apart: 9, of which 3 were waited for; matrix products, arithmetic and copies ran while one was open for 0% of the time, Pallas kernels for 26%

profile of v1, /device:TPU:0, one launch (start us, length us, event | category | flops | bytes accessed | tf_op | source)
XLA Modules:
  0.0 244.1 jit_solution(9770182811735800896)
XLA Ops:
  0.0 1.6 copy.17
  1.6 3.4 %collective-permute-start.1 = (f32[2,2,96,160]{3,2,1,0:T(8,128)S(1)}, f32[2,2,96,160]{3,2,1,0:T(8,128)S(1)}, u32[]{:S(2)}, u32[]{:S(2)}) collective-permute-start(f32[2,2,96,160]{3,2,1,0:T(8,128)S(1)} %slice.13), channel_id=1, source_target_pairs={{1,0},{2,1},{3,2},{4,3},{5,4},{6,5},{7,6},{0,7},{9,8},{10,9},{11,1... | collective-permute-start | bytes 737288 | tf_op jit(solution)/shard_map/ppermute | solution.py:91
  5.2 9.0 %collective-permute-done.before_ref = f32[2,2,64,160]{3,2,1,0:T(8,128)S(1)} collective-permute-done((f32[2,2,64,160]{3,2,1,0:T(8,128)S(1)}, f32[2,2,64,160]{3,2,1,0:T(8,128)S(1)}, u32[]{:S(2)}, u32[]{:S(2)}) %collective-permute-start) | collective-permute-done | bytes 163872 | tf_op jit(solution)/shard_map/ppermute | solution.py:90
  14.2 18.5 %advect.1 = f32[8,320,128]{2,1,0:T(8,128)S(1)} custom-call(f32[2,2,320,160]{3,2,1,0:T(8,128)S(1)} %bitcast.21, f32[2,2,64,160]{3,2,1,0:T(8,128)S(1)} %collective-permute-done.before_ref, f32[2,2,96,160]{3,2,1,0:T(8,128)S(1)} %collective-permute-done.1.after_ref, s32[2,10,1,160]{3,2,1,0:T(1,128)S(1)} %copy.18.depart_ref, bf16[2,10,64,32,160]{4,3,2,1,0:T(8,128)(2,1)} %bitcast.25), custom_call_target="tpu_custom_call" | custom-call | flops 209715200 | bytes 19660800 | tf_op jit(solution)/shard_map/advect/pallas_call | solution.py:94
  32.7 20.6 %all_to_all.20 = f32[8,320,128]{2,1,0:T(8,128)S(1)} all-to-all(f32[8,320,128]{2,1,0:T(8,128)S(1)} %advect.1), channel_id=1, replica_groups=mesh['band'=4,'sector'=8] {'sector'}, dimensions={0} | all-to-all | bytes 2621440 | tf_op jit(solution)/shard_map/all_to_all | solution.py:453
  54.7 4.0 %forward.1 = f32[2560,128]{1,0:T(8,128)} custom-call(f32[2560,128]{1,0:T(8,128)S(1)} %bitcast.22, bf16[640,640]{1,0:T(8,128)(2,1)S(1)} %copy-done.5, bf16[640,640]{1,0:T(8,128)(2,1)S(1)} %copy-done.6, f32[5,2,320,128]{3,2,1,0:T(8,128)S(1)} %broadcast_in_dim.10.twiddle_ref), custom_call_target="tpu_custom_call" | custom-call | flops 2516582400 | bytes 5242880 | tf_op jit(solution)/shard_map/forward/pallas_call | solution.py:237
  58.7 3.6 %all-to-all-start.1 = ((f32[8,320,128]{2,1,0:T(8,128)}), f32[8,320,128]{2,1,0:T(8,128)S(1)}, u32[]{:S(2)}, u32[]{:S(2)}) async-start(f32[8,320,128]{2,1,0:T(8,128)} %bitcast.10), calls=%async_computation.1 | async-start | bytes 2621440 | tf_op jit(solution)/shard_map/all_to_all | solution.py:453
  62.4 18.0 %all-to-all-done.1.z_ref = f32[8,320,128]{2,1,0:T(8,128)S(1)} async-done(((f32[8,320,128]{2,1,0:T(8,128)}), f32[8,320,128]{2,1,0:T(8,128)S(1)}, u32[]{:S(2)}, u32[]{:S(2)}) %all-to-all-start.1) | async-done | bytes 1310752 | tf_op jit(solution)/shard_map/all_to_all | solution.py:453
  80.4 11.4 %analyse.4 = f32[10,8,1281]{2,1,0:T(8,128)S(1)} custom-call(s32[2]{0:T(128)S(1)} %pad_add_fusion.3.place_ref, f32[8,320,128]{2,1,0:T(8,128)S(1)} %all-to-all-done.1.z_ref, f32[80,160,1281]{2,1,0:T(8,128)} %legendre_ref.15), custom_call_target="tpu_custom_call" | custom-call | flops 1311744000 | bytes 16396800 | tf_op jit(solution)/shard_map/analyse/pallas_call | solution.py:306
  91.8 1.6 collective-permute-start.2
  93.5 11.4 %analyse.5 = f32[10,8,1281]{2,1,0:T(8,128)S(1)} custom-call(s32[2]{0:T(128)S(1)} %get-tuple-element.10.place_ref, f32[8,320,128]{2,1,0:T(8,128)S(1)} %all-to-all-done.1.z_ref, f32[80,160,1281]{2,1,0:T(8,128)} %legendre_ref.15), custom_call_target="tpu_custom_call" | custom-call | flops 1311744000 | bytes 16396800 | tf_op jit(solution)/shard_map/analyse/pallas_call | solution.py:306
  104.9 11.4 %analyse.6 = f32[10,8,1281]{2,1,0:T(8,128)S(1)} custom-call(s32[2]{0:T(128)S(1)} %get-tuple-element.11.place_ref, f32[8,320,128]{2,1,0:T(8,128)S(1)} %all-to-all-done.1.z_ref, f32[80,160,1281]{2,1,0:T(8,128)} %legendre_ref.15), custom_call_target="tpu_custom_call" | custom-call | flops 1311744000 | bytes 16396800 | tf_op jit(solution)/shard_map/analyse/pallas_call | solution.py:306
  116.8 2.6 %collective-permute-start.5 = (f32[10,8,1281]{2,1,0:T(8,128)S(1)}, f32[10,8,1281]{2,1,0:T(8,128)S(1)}, u32[]{:S(2)}, u32[]{:S(2)}) collective-permute-start(f32[10,8,1281]{2,1,0:T(8,128)S(1)} %add.27), channel_id=1, source_target_pairs={{0,16},{8,24},{16,0},{24,8},{1,17},{9,25},{17,1},{25,9},{2,18},{10... | collective-permute-start | bytes 1229768 | tf_op jit(solution)/shard_map/ppermute | solution.py:417
  119.5 11.4 %analyse.7 = f32[10,8,1281]{2,1,0:T(8,128)S(1)} custom-call(s32[2]{0:T(128)S(1)} %pad_add_fusion.1.place_ref, f32[8,320,128]{2,1,0:T(8,128)S(1)} %all-to-all-done.1.z_ref, f32[80,160,1281]{2,1,0:T(8,128)} %legendre_ref.15), custom_call_target="tpu_custom_call" | custom-call | flops 1311744000 | bytes 16396800 | tf_op jit(solution)/shard_map/analyse/pallas_call | solution.py:306
  130.9 4.1 %collective-permute-done.3 = f32[10,8,1281]{2,1,0:T(8,128)S(1)} collective-permute-done((f32[10,8,1281]{2,1,0:T(8,128)S(1)}, f32[10,8,1281]{2,1,0:T(8,128)S(1)}, u32[]{:S(2)}, u32[]{:S(2)}) %collective-permute-start.3) | collective-permute-done | bytes 409952 | tf_op jit(solution)/shard_map/ppermute | solution.py:417
  135.1 5.2 %collective-permute-start.6 = (f32[10,8,1281]{2,1,0:T(8,128)S(1)}, f32[10,8,1281]{2,1,0:T(8,128)S(1)}, u32[]{:S(2)}, u32[]{:S(2)}) collective-permute-start(f32[10,8,1281]{2,1,0:T(8,128)S(1)} %add.29.spectrum_ref), channel_id=1, source_target_pairs={{0,8},{8,0},{16,24},{24,16},{1,9},{9,1},{17,25},{25,17},{2,10},{10... | collective-permute-start | bytes 1229768 | tf_op jit(solution)/shard_map/ppermute | solution.py:417
  141.2 13.4 %synthesise.4.rest_0_ = f32[8,320,128]{2,1,0:T(8,128)S(1)} custom-call(s32[2]{0:T(128)S(1)} %get-tuple-element.10.place_ref, f32[2]{0:T(128)S(1)} %copy-done.2, f32[10,8,1281]{2,1,0:T(8,128)S(1)} %add.29.spectrum_ref, f32[80,160,1281]{2,1,0:T(8,128)} %legendre_ref.15), custom_call_target="tpu_custom_call" | custom-call | flops 1311744000 | bytes 16396800 | tf_op jit(solution)/shard_map/synthesise/pallas_call | solution.py:388
  154.6 13.4 %synthesise.5.rest_0_ = f32[8,320,128]{2,1,0:T(8,128)S(1)} custom-call(s32[2]{0:T(128)S(1)} %pad_add_fusion.3.place_ref, f32[2]{0:T(128)S(1)} %copy-done.2, f32[10,8,1281]{2,1,0:T(8,128)S(1)} %collective-permute-done.6.spectrum_ref, f32[80,160,1281]{2,1,0:T(8,128)} %legendre_ref.15, f32[8,320,128]{2,1,0:T(8,128)S(1)} %synthesise.4.rest_0_), custom_call_target="tpu_custom_call", output_to_operand_aliasing={{}: (4, {})} | custom-call | flops 1311744000 | bytes 16396800 | tf_op jit(solution)/shard_map/synthesise/pallas_call | solution.py:388
  168.2 13.4 %synthesise.6.rest_0_ = f32[8,320,128]{2,1,0:T(8,128)S(1)} custom-call(s32[2]{0:T(128)S(1)} %pad_add_fusion.1.place_ref, f32[2]{0:T(128)S(1)} %copy-done.2, f32[10,8,1281]{2,1,0:T(8,128)S(1)} %add.30.spectrum_ref, f32[80,160,1281]{2,1,0:T(8,128)} %legendre_ref.15, f32[8,320,128]{2,1,0:T(8,128)S(1)} %synthesise.5.rest_0_), custom_call_target="tpu_custom_call", output_to_operand_aliasing={{}: (4, {})} | custom-call | flops 1311744000 | bytes 16396800 | tf_op jit(solution)/shard_map/synthesise/pallas_call | solution.py:388
  181.6 13.4 %synthesise.7 = f32[8,320,128]{2,1,0:T(8,128)S(1)} custom-call(s32[2]{0:T(128)S(1)} %get-tuple-element.11.place_ref, f32[2]{0:T(128)S(1)} %copy-done.2, f32[10,8,1281]{2,1,0:T(8,128)S(1)} %collective-permute-done.7.spectrum_ref, f32[80,160,1281]{2,1,0:T(8,128)} %legendre_ref.15, f32[8,320,128]{2,1,0:T(8,128)S(1)} %synthesise.6.rest_0_), custom_call_target="tpu_custom_call", output_to_operand_aliasing={{}: (4, {})} | custom-call | flops 1311744000 | bytes 16396800 | tf_op jit(solution)/shard_map/synthesise/pallas_call | solution.py:388
  195.0 24.7 %all_to_all.21 = f32[8,320,128]{2,1,0:T(8,128)S(1)} all-to-all(f32[8,320,128]{2,1,0:T(8,128)S(1)} %synthesise.7), channel_id=1, replica_groups=mesh['band'=4,'sector'=8] {'sector'}, dimensions={0} | all-to-all | bytes 2621440 | tf_op jit(solution)/shard_map/all_to_all | solution.py:453
  219.7 2.4 inverse.1
  222.1 20.6 %all_to_all.22 = f32[8,320,128]{2,1,0:T(8,128)S(1)} all-to-all(f32[8,320,128]{2,1,0:T(8,128)S(1)} %bitcast.24), channel_id=1, replica_groups=mesh['band'=4,'sector'=8] {'sector'}, dimensions={0} | all-to-all | bytes 2621440 | tf_op jit(solution)/shard_map/all_to_all | solution.py:453
  242.7 1.4 copy.19
  (39 shorter events, 3.5 us)
Async XLA Ops:
  0.0 5.1 %copy-start.7 = (s32[2,160,10]{1,0,2:T(2,128)S(1)}, s32[2,160,10]{1,0,2:T(2,128)}, u32[]{:S(2)}) copy-start(s32[2,160,10]{1,0,2:T(2,128)} %param.11) | copy-start | bytes 38404
  1.6 12.5 %collective-permute-start.1 = (f32[2,2,96,160]{3,2,1,0:T(8,128)S(1)}, f32[2,2,96,160]{3,2,1,0:T(8,128)S(1)}, u32[]{:S(2)}, u32[]{:S(2)}) collective-permute-start(f32[2,2,96,160]{3,2,1,0:T(8,128)S(1)} %slice.13), channel_id=1, source_target_pairs={{1,0},{2,1},{3,2},{4,3},{5,4},{6,5},{7,6},{0,7},{9,8},{10,9},{11,1... | collective-permute-start | bytes 737288 | tf_op jit(solution)/shard_map/ppermute | solution.py:91
  5.1 9.1 %collective-permute-start = (f32[2,2,64,160]{3,2,1,0:T(8,128)S(1)}, f32[2,2,64,160]{3,2,1,0:T(8,128)S(1)}, u32[]{:S(2)}, u32[]{:S(2)}) collective-permute-start(f32[2,2,64,160]{3,2,1,0:T(8,128)S(1)} %slice.12), channel_id=1, source_target_pairs={{0,1},{1,2},{2,3},{3,4},{4,5},{5,6},{6,7},{7,0},{8,9},{9,10},{10,1... | collective-permute-start | bytes 491528 | tf_op jit(solution)/shard_map/ppermute | solution.py:90
  32.7 20.6 %copy-start.8 = (f32[5,2,320]{2,1,0:T(2,128)S(1)}, f32[5,2,320]{2,1,0:T(2,128)}, u32[]{:S(2)}) copy-start(f32[5,2,320]{2,1,0:T(2,128)} %constant.38.clone) | copy-start | bytes 38404
  53.3 1.1 copy-start.5
  53.3 1.4 copy-start.6
  54.7 4.0 %copy-start = (f32[5,2,320,128]{3,2,1,0:T(8,128)}, f32[5,2,320,128]{3,2,1,0:T(8,128)S(1)}, u32[]{:S(2)}) copy-start(f32[5,2,320,128]{3,2,1,0:T(8,128)S(1)} %broadcast_in_dim.10.twiddle_ref) | copy-start | bytes 4915204
  58.7 21.7 %all-to-all-start.1 = ((f32[8,320,128]{2,1,0:T(8,128)}), f32[8,320,128]{2,1,0:T(8,128)S(1)}, u32[]{:S(2)}, u32[]{:S(2)}) async-start(f32[8,320,128]{2,1,0:T(8,128)} %bitcast.10), calls=%async_computation.1 | async-start | bytes 2621440 | tf_op jit(solution)/shard_map/all_to_all | solution.py:453
  91.8 13.1 %collective-permute-start.2 = (f32[10,8,1281]{2,1,0:T(8,128)S(1)}, f32[10,8,1281]{2,1,0:T(8,128)S(1)}, u32[]{:S(2)}, u32[]{:S(2)}) collective-permute-start(f32[10,8,1281]{2,1,0:T(8,128)S(1)} %analyse.4), channel_id=1, source_target_pairs={{0,8},{8,0},{16,24},{24,16},{1,9},{9,1},{17,25},{25,17},{2,10},{10... | collective-permute-start | bytes 1229768 | tf_op jit(solution)/shard_map/ppermute | solution.py:417
  116.3 18.7 %collective-permute-start.3 = (f32[10,8,1281]{2,1,0:T(8,128)S(1)}, f32[10,8,1281]{2,1,0:T(8,128)S(1)}, u32[]{:S(2)}, u32[]{:S(2)}) collective-permute-start(f32[10,8,1281]{2,1,0:T(8,128)S(1)} %analyse.6), channel_id=1, source_target_pairs={{0,8},{8,0},{16,24},{24,16},{1,9},{9,1},{17,25},{25,17},{2,10},{10... | collective-permute-start | bytes 1229768 | tf_op jit(solution)/shard_map/ppermute | solution.py:417
  116.8 18.2 %collective-permute-start.5 = (f32[10,8,1281]{2,1,0:T(8,128)S(1)}, f32[10,8,1281]{2,1,0:T(8,128)S(1)}, u32[]{:S(2)}, u32[]{:S(2)}) collective-permute-start(f32[10,8,1281]{2,1,0:T(8,128)S(1)} %add.27), channel_id=1, source_target_pairs={{0,16},{8,24},{16,0},{24,8},{1,17},{9,25},{17,1},{25,9},{2,18},{10... | collective-permute-start | bytes 1229768 | tf_op jit(solution)/shard_map/ppermute | solution.py:417
  130.9 10.3 %copy-start.2 = (f32[2]{0:T(128)S(1)}, f32[2]{0:T(128)}, u32[]{:S(2)}) copy-start(f32[2]{0:T(128)} %damping_ref.7) | copy-start | bytes 28
  135.1 19.4 %collective-permute-start.6 = (f32[10,8,1281]{2,1,0:T(8,128)S(1)}, f32[10,8,1281]{2,1,0:T(8,128)S(1)}, u32[]{:S(2)}, u32[]{:S(2)}) collective-permute-start(f32[10,8,1281]{2,1,0:T(8,128)S(1)} %add.29.spectrum_ref), channel_id=1, source_target_pairs={{0,8},{8,0},{16,24},{24,16},{1,9},{9,1},{17,25},{25,17},{2,10},{10... | collective-permute-start | bytes 1229768 | tf_op jit(solution)/shard_map/ppermute | solution.py:417
  140.3 27.6 %collective-permute-start.4 = (f32[10,8,1281]{2,1,0:T(8,128)S(1)}, f32[10,8,1281]{2,1,0:T(8,128)S(1)}, u32[]{:S(2)}, u32[]{:S(2)}) collective-permute-start(f32[10,8,1281]{2,1,0:T(8,128)S(1)} %add.28), channel_id=1, source_target_pairs={{0,16},{8,24},{16,0},{24,8},{1,17},{9,25},{17,1},{25,9},{2,18},{10... | collective-permute-start | bytes 1229768 | tf_op jit(solution)/shard_map/ppermute | solution.py:417
  168.1 13.5 %collective-permute-start.7 = (f32[10,8,1281]{2,1,0:T(8,128)S(1)}, f32[10,8,1281]{2,1,0:T(8,128)S(1)}, u32[]{:S(2)}, u32[]{:S(2)}) collective-permute-start(f32[10,8,1281]{2,1,0:T(8,128)S(1)} %add.30.spectrum_ref), channel_id=1, source_target_pairs={{0,8},{8,0},{16,24},{24,16},{1,9},{9,1},{17,25},{25,17},{2,10},{10... | collective-permute-start | bytes 1229768 | tf_op jit(solution)/shard_map/ppermute | solution.py:417
  181.6 38.1 %copy-start.4 = (bf16[640,640]{1,0:T(8,128)(2,1)S(1)}, bf16[640,640]{1,0:T(8,128)(2,1)}, u32[]{:S(2)}) copy-start(bf16[640,640]{1,0:T(8,128)(2,1)} %constant.42.clone.low_ref) | copy-start | bytes 2457604
  195.0 24.7 %copy-start.1 = (f32[5,2,320,128]{3,2,1,0:T(8,128)S(1)}, f32[5,2,320,128]{3,2,1,0:T(8,128)}, u32[]{:S(2)}) copy-start(f32[5,2,320,128]{3,2,1,0:T(8,128)} %copy-done) | copy-start | bytes 4915204
  195.0 24.7 %copy-start.3 = (bf16[640,640]{1,0:T(8,128)(2,1)S(1)}, bf16[640,640]{1,0:T(8,128)(2,1)}, u32[]{:S(2)}) copy-start(bf16[640,640]{1,0:T(8,128)(2,1)} %constant.41.clone.high_ref) | copy-start | bytes 2457604

commit v2 on v1

v2 whole, which is shorter than its diff:
```python
import functools
import math

import jax
import jax.numpy as jnp
import numpy as np
from jax import lax
from jax.experimental import pallas as pl
from jax.experimental.pallas import tpu as pltpu
from jax.sharding import PartitionSpec as P


REACH_BACK = 2
REACH_AHEAD = 3
CHUNKS = 4
SPLITS = 2
INNER = 5
LANES = 128
UNIT = 64
RADIX = 16
DEPTH = 6
WEIGHT = 2
WIDE = 256
F32 = jnp.float32
BF16 = jnp.bfloat16


def params(*semantics):
    return pltpu.CompilerParams(dimension_semantics=semantics, vmem_limit_bytes=48 * 1024 * 1024)


def cost(flops, moved):
    return pl.CostEstimate(flops=int(flops), bytes_accessed=int(moved), transcendentals=0)


def split(x):
    high = x.astype(BF16)
    low = (x - high.astype(F32)).astype(BF16)
    return high, low


def split_np(x):
    high = np.asarray(x, np.float32).astype(jnp.bfloat16)
    low = (np.asarray(x, np.float64) - high.astype(np.float64)).astype(np.float32).astype(jnp.bfloat16)
    return high, low


def stream(step, steps, depth, copies):
    ahead = depth - 1

    @pl.when(step == 0)
    def _():
        for early in range(min(ahead, steps)):
            for copy in copies(early, early):
                copy.start()

    @pl.when(step + ahead < steps)
    def _():
        for copy in copies(step + ahead, lax.rem(step + ahead, depth)):
            copy.start()

    slot = lax.rem(step, depth)
    for copy in copies(step, slot):
        copy.wait()
    return slot


def piece_widths(share):
    return [w for w in (64, 32, 16) if share & w]


def packable(share, rows, lanes=LANES):
    return share < lanes and share % 16 == 0 and rows % UNIT == 0


def packed_rows(rows, share):
    return rows * share // LANES


def pack(x, share):
    rows, offset, blocks = x.shape[0], 0, []
    for w in piece_widths(share):
        folds = LANES // w
        h = rows // folds
        blocks.append(jnp.concatenate([x[b * h : (b + 1) * h, offset : offset + w] for b in range(folds)], axis=1))
        offset += w
    return jnp.concatenate(blocks, axis=0)


def unpack(y, share):
    rows = y.shape[0] * LANES // share
    first, columns = 0, []
    for w in piece_widths(share):
        folds = LANES // w
        h = rows // folds
        block = y[first : first + h]
        columns.append(jnp.concatenate([block[:, b * w : (b + 1) * w] for b in range(folds)], axis=0))
        first += h
    columns.append(jnp.zeros((rows, LANES - share), y.dtype))
    return jnp.concatenate(columns, axis=1)


def advect_kernel(groups_ref, *refs, width, parts, share, group, count, packed, halo):
    if halo:
        field_ref, before_ref, after_ref, depart_ref, weight_ref, _, out_ref, extended, window, weights, sems = refs
    else:
        field_ref, depart_ref, weight_ref, out_ref, extended, window, weights, sems = refs
    hemi, place = pl.program_id(0), pl.program_id(1)
    levels, local, columns = field_ref.shape[1], field_ref.shape[2], field_ref.shape[3]
    back, ahead = REACH_BACK * width, REACH_AHEAD * width

    @pl.when(place == 0)
    def _():
        for v in range(levels):
            extended[v, back : back + local] = field_ref[0, v]
            if halo:
                extended[v, 0:back] = before_ref[0, v]
                extended[v, back + local : back + local + ahead] = after_ref[0, v]

    def copies(step, slot):
        tiles = groups_ref[lax.rem(step, count)] * group
        source = lax.div(step, count)
        return [
            pltpu.make_async_copy(weight_ref.at[source, tiles + n], weights.at[slot, n], sems.at[slot, n])
            for n in range(group)
        ]

    slot = stream(hemi * count + place, 2 * count, DEPTH, copies)
    results = [[] for _ in range(levels)]
    for n in range(group):
        tile = groups_ref[place] * group + n
        depart = depart_ref[0, n]
        start = pl.multiple_of(tile * width, width)
        for v in range(levels):
            for half in range(0, 2 * width, 8):
                picked = None
                for step in range(2 * REACH_BACK + 1):
                    rows = extended[v, pl.ds(start + step * width + half, 8), :]
                    chosen = depart == (step - REACH_BACK)
                    picked = rows if picked is None else jnp.where(chosen, rows, picked)
                window[v, half : half + 8] = picked

        def body(block, totals):
            for j in range(8):
                row = block * 8 + j
                weight = weights[slot, n, row].astype(F32)
                totals = tuple(totals[v] + window[v, pl.ds(row, 1), :] * weight for v in range(levels))
            return totals

        zero = jnp.zeros((width, columns), F32)
        totals = lax.fori_loop(0, 2 * width // 8, body, (zero,) * levels)
        for v in range(levels):
            results[v].append(totals[v])
    for v in range(levels):
        value = jnp.concatenate(results[v], axis=0)
        for part in range(parts):
            mine = value[:, part * share : (part + 1) * share]
            if packed:
                out_ref[v * parts + part] = pack(mine, share)
            else:
                out_ref[v * parts + part, :, 0:share] = mine


def advect(field, depart, interp_weight, sectors):
    hemis, lats, levels, local = field.shape
    width = interp_weight.shape[-1]
    tiles = depart.shape[2]
    parts = sectors // (hemis * levels)
    share = lats // parts
    packed = packable(share, local) and UNIT % width == 0
    group = UNIT // width if packed else 1
    rows = packed_rows(group * width, share) if packed else width
    turned = jnp.transpose(field, (0, 2, 3, 1))
    up = [(i, (i + 1) % sectors) for i in range(sectors)]
    down = [(j, i) for i, j in up]
    before = lax.ppermute(turned[:, :, local - REACH_BACK * width :], "sector", up)
    after = lax.ppermute(turned[:, :, : REACH_AHEAD * width], "sector", down)
    weights = jnp.transpose(interp_weight, (0, 2, 3, 4, 1))
    offsets = jnp.transpose(depart, (0, 2, 1))[:, :, None, :]
    every = list(range(tiles // group))
    inner = [g for g in every if g * group >= REACH_BACK and (g + 1) * group - 1 + REACH_AHEAD < tiles]
    outer = [g for g in every if g not in inner]

    def call(groups, halo, previous):
        count = len(groups)
        field_specs = [pl.BlockSpec((1, levels, local, lats), lambda h, g, groups: (h, 0, 0, 0))]
        operands = [jnp.asarray(groups, jnp.int32), turned]
        if halo:
            for side in (before, after):
                field_specs.append(pl.BlockSpec((1,) + side.shape[1:], lambda h, g, groups: (h, 0, 0, 0)))
                operands.append(side)
        operands += [offsets, weights]
        in_specs = field_specs + [
            pl.BlockSpec((1, group, 1, lats), lambda h, g, groups: (h, groups[g], 0, 0)),
            pl.BlockSpec(memory_space=pl.ANY),
        ]
        aliases = {}
        if halo:
            operands.append(previous)
            in_specs.append(pl.BlockSpec(memory_space=pl.ANY))
            aliases = {len(operands) - 1: 0}
        return pl.pallas_call(
            functools.partial(advect_kernel, width=width, parts=parts, share=share, group=group, count=count, packed=packed, halo=halo),
            grid_spec=pltpu.PrefetchScalarGridSpec(
                num_scalar_prefetch=1,
                grid=(hemis, count),
                in_specs=in_specs,
                out_specs=pl.BlockSpec((levels * parts, rows, LANES), lambda h, g, groups: (h, groups[g], 0)),
                scratch_shapes=[
                    pltpu.VMEM((levels, local + (REACH_BACK + REACH_AHEAD) * width, lats), F32),
                    pltpu.VMEM((levels, 2 * width, lats), F32),
                    pltpu.VMEM((DEPTH, group, 2 * width, width, lats), BF16),
                    pltpu.SemaphoreType.DMA((DEPTH, group)),
                ],
            ),
            out_shape=jax.ShapeDtypeStruct((sectors, rows * len(every), LANES), F32),
            input_output_aliases=aliases,
            compiler_params=params("arbitrary", "arbitrary"),
            cost_estimate=cost(4 * hemis * count * group * levels * 2 * width * width * lats * 4, interp_weight.size * 3 * count // len(every)),
            name="advect_edge" if halo else "advect_inner",
        )(*operands)

    if inner:
        result = call(inner, False, None)
    else:
        result = jnp.zeros((sectors, rows * len(every), LANES), F32)
    return call(outer, True, result), packed, share


def fourier_tables(lon_count, radix):
    inner = lon_count // radix
    waves = lon_count // 2
    slots = waves // 2 // radix
    index = np.arange(slots)
    direct = index
    mirror = waves // radix - 1 - index
    rows = []
    for kind in range(2):
        for component in range(4):
            degree = direct if component < 2 else mirror
            source = degree if kind == 0 else inner - 1 - degree
            angle = 2.0 * np.pi * ((source[:, None] * np.arange(inner)[None, :]) % inner) / inner
            if component % 2 == 0:
                row = np.concatenate([np.cos(angle), np.sin(angle)], axis=1)
            else:
                sign = 1.0 if kind == 0 else -1.0
                row = sign * np.concatenate([-np.sin(angle), np.cos(angle)], axis=1)
            rows.append(row)
    matrix = np.concatenate(rows, axis=0)
    order = np.arange(radix // 2 + 1)[:, None] * np.arange(inner)[None, :]
    angle = 2.0 * np.pi * (order % lon_count) / lon_count
    twiddle = np.stack([np.cos(angle), -np.sin(angle)], axis=1).astype(np.float32)
    return matrix, twiddle


def scaled(x, factor):
    if abs(factor - 1.0) < 1e-12:
        return x
    if abs(factor + 1.0) < 1e-12:
        return -x
    return x * np.float32(factor)


def combine(terms):
    total = None
    for factor, x in terms:
        if abs(factor) < 1e-12:
            continue
        total = scaled(x, factor) if total is None else total + scaled(x, factor)
    return total


def products(high_ref, low_ref, rows, depth, x):
    x_high, x_low = split(x)
    both = jnp.concatenate([x_high, x_low], axis=1)
    first = jnp.dot(high_ref[0:rows, 0:depth], both, preferred_element_type=F32)
    second = jnp.dot(low_ref[0:rows, 0:depth], x_high, preferred_element_type=F32)
    return first[:, 0:LANES] + first[:, LANES:] + second


def places(a, radix):
    residues = [a] if a in (0, radix // 2) else [a, radix - a]
    result = []
    for residue in residues:
        for component in range(4):
            first = residue if component < 2 else radix - 1 - residue
            result.append(first * 4 + component)
    return result


def chunk_rows(rows, sectors):
    n = rows // (sectors * 2 * SPLITS)
    return [(block * n, block * n * SPLITS, n) for block in range(sectors * 2)]


def forward_kernel(x_ref, high_ref, low_ref, twiddle_ref, *refs, radix, share, rows, sectors):
    outs, scratch = refs[:SPLITS], refs[SPLITS:]
    inner = rows // radix
    slots = rows // (4 * radix)
    out_ref = scratch[0]
    if len(scratch) > 1:
        plain = scratch[1]
        short = packed_rows(UNIT, share)
        for unit in range(rows // UNIT):
            plain[unit * UNIT : (unit + 1) * UNIT] = unpack(x_ref[unit * short : (unit + 1) * short], share)
    else:
        plain = x_ref
    x = [plain[s * inner : (s + 1) * inner] for s in range(radix)]
    middle = radix // 2
    even = {s: x[s] + x[radix - s] for s in range(1, middle)}
    odd = {s: x[s] - x[radix - s] for s in range(1, middle)}
    for a in range(middle + 1):
        angle = [2.0 * math.pi * ((a * s) % radix) / radix for s in range(radix)]
        real = combine([(1.0, x[0]), (math.cos(angle[middle]), x[middle])] + [(math.cos(angle[s]), even[s]) for s in even])
        imag = combine([(-math.sin(angle[s]), odd[s]) for s in odd])
        where = places(a, radix)
        if a == 0:
            result = products(high_ref, low_ref, len(where) * slots, inner, real)
        else:
            cos, sin = twiddle_ref[a, 0], twiddle_ref[a, 1]
            turned_real = cos * real if imag is None else cos * real - sin * imag
            turned_imag = sin * real if imag is None else sin * real + cos * imag
            turned = jnp.concatenate([turned_real, turned_imag], axis=0)
            result = products(high_ref, low_ref, len(where) * slots, 2 * inner, turned)
        for n, first in enumerate(where):
            out_ref[pl.ds(first, slots, stride=4 * radix), :] = result[n * slots : (n + 1) * slots]
    for target, source, n in chunk_rows(rows, sectors):
        for c in range(SPLITS):
            outs[c][target : target + n] = out_ref[source + c * n : source + (c + 1) * n]


def inverse_kernel(*refs, radix, share, rows, sectors):
    ins, (high_ref, low_ref, twiddle_ref, final_ref, z_ref, *scratch) = refs[:SPLITS], refs[SPLITS:]
    out_ref = scratch[0] if scratch else final_ref
    inner = rows // radix
    slots = rows // (4 * radix)
    for source, target, n in chunk_rows(rows, sectors):
        for c in range(SPLITS):
            z_ref[target + c * n : target + (c + 1) * n] = ins[c][source : source + n]
    middle = radix // 2
    reals, imags = [], []
    for a in range(middle + 1):
        where = places(a, radix)
        pieces = [z_ref[pl.ds(first, slots, stride=4 * radix), :] for first in where]
        if a == 0:
            row = lax.broadcasted_iota(jnp.int32, pieces[0].shape, 0)
            pieces[0] = jnp.where(row == 0, 0.5 * pieces[0], pieces[0])
        column = jnp.concatenate(pieces, axis=0)
        depth = len(where) * slots
        if a == 0:
            reals.append(products(high_ref, low_ref, inner, depth, column))
            imags.append(None)
            continue
        result = products(high_ref, low_ref, 2 * inner, depth, column)
        real, imag = result[0:inner], result[inner:]
        cos, sin = twiddle_ref[a, 0], twiddle_ref[a, 1]
        reals.append(cos * real + sin * imag)
        imags.append(None if a == middle else cos * imag - sin * real)
    for s in range(middle + 1):
        angle = [2.0 * math.pi * ((a * s) % radix) / radix for a in range(middle + 1)]
        even = combine([(math.cos(angle[a]), reals[a]) for a in range(middle + 1)])
        odd = combine([(-math.sin(angle[a]), imags[a]) for a in range(1, middle)])
        if s == 0 or s == middle:
            out_ref[s * inner : (s + 1) * inner] = even
        else:
            out_ref[s * inner : (s + 1) * inner] = even + odd
            other = radix - s
            out_ref[other * inner : (other + 1) * inner] = even - odd
    if scratch:
        short = packed_rows(UNIT, share)
        for unit in range(rows // UNIT):
            final_ref[unit * short : (unit + 1) * short] = pack(out_ref[unit * UNIT : (unit + 1) * UNIT], share)


def finish_kernel(x_ref, out_ref, plain, *, levels, parts, share):
    short = packed_rows(UNIT, share)
    for v in range(levels):
        for part in range(parts):
            for unit in range(plain.shape[0] // UNIT):
                block = x_ref[v * parts + part, unit * short : (unit + 1) * short]
                plain[unit * UNIT : (unit + 1) * UNIT, part * share : (part + 1) * share] = unpack(block, share)[:, 0:share]
        out_ref[0, :, v, :] = jnp.transpose(plain[...], (1, 0))


def finish(x, hemis, lats, levels, local, share):
    sectors, rows, _ = x.shape
    each = sectors // hemis
    return pl.pallas_call(
        functools.partial(finish_kernel, levels=levels, parts=each // levels, share=share),
        grid=(hemis,),
        in_specs=[pl.BlockSpec((each, rows, LANES), lambda h: (h, 0, 0))],
        out_specs=pl.BlockSpec((1, lats, levels, local), lambda h: (h, 0, 0, 0)),
        out_shape=jax.ShapeDtypeStruct((hemis, lats, levels, local), F32),
        scratch_shapes=[pltpu.VMEM((local, lats), F32)],
        compiler_params=params("arbitrary"),
        name="finish",
    )(x)


def transform(kernel, inputs, tables, out_rows, scratch_rows, **settings):
    matrix = tables[0]
    outs = tuple(jax.ShapeDtypeStruct((n, LANES), F32) for n in out_rows)
    return pl.pallas_call(
        functools.partial(kernel, **settings),
        out_shape=outs,
        scratch_shapes=[pltpu.VMEM((n, LANES), F32) for n in scratch_rows],
        compiler_params=pltpu.CompilerParams(vmem_limit_bytes=48 * 1024 * 1024),
        cost_estimate=cost(3 * 2 * matrix.size * LANES * settings["radix"], 8 * sum(out_rows) * LANES),
    )(*inputs, *tables)


def row_masks(pair, waves, shape, first):
    column = first + lax.broadcasted_iota(jnp.int32, shape, 1)
    limit = waves - pair
    leading = column < limit
    lag = jnp.where(leading, column, column - limit)
    odd = (lag & 1) == 1
    return column, leading, odd


def ranges(count):
    edges = list(range(0, count - count % WIDE, WIDE)) + [count]
    return list(zip(edges[:-1], edges[1:]))


def gather_lats(z_ref, hemi, level, levels, parts, share, start):
    rows = [z_ref[(hemi * levels + level) * parts + part, pl.ds(start, 8), 0:share] for part in range(parts)]
    return jnp.concatenate(rows, axis=1)


def legendre_stream(place_ref, legendre_ref, buffer, sems, step, steps):
    def copies(step, slot):
        pair = 2 * (place_ref[0] + step)
        return [
            pltpu.make_async_copy(legendre_ref.at[pair + n], buffer.at[slot, n], sems.at[slot, n]) for n in range(2)
        ]

    return stream(step, steps, DEPTH, copies)


def analyse_kernel(place_ref, z_ref, legendre_ref, out_ref, buffer, sems, *, levels, parts, share, steps):
    inner = out_ref.shape[0]
    count = legendre_ref.shape[2]
    waves = count - 1

    def body(index, carry):
        local_step = pl.program_id(0) * inner + index
        slot = legendre_stream(place_ref, legendre_ref, buffer, sems, local_step, steps)
        start = pl.multiple_of((place_ref[2] + local_step) * 8, 8)
        sums, differences = [], []
        for v in range(levels):
            north = gather_lats(z_ref, 0, v, levels, parts, share, start)
            south = gather_lats(z_ref, 1, v, levels, parts, share, start)
            sums.append(north + south)
            differences.append(north - south)
        stacks = []
        for which in range(2):
            low, high = which * 4, which * 4 + 4
            wave = jnp.concatenate([x[low:high] for x in sums + differences], axis=0)
            wave_high, wave_low = split(wave)
            stacks.append((jnp.concatenate([wave_high, wave_low], axis=0), wave_high))
        for first, last in ranges(count):
            picked = []
            for which in range(2):
                both, wave_high = stacks[which]
                rows = both.shape[0] // 2
                high, low = split(buffer[slot, which, :, first:last])
                product = jnp.dot(both, high, preferred_element_type=F32)
                product = product[0:rows] + product[rows:] + jnp.dot(wave_high, low, preferred_element_type=F32)
                pair = place_ref[1] + 2 * (place_ref[0] + local_step) + which
                shape = (rows // 2, last - first)
                _, leading, odd = row_masks(pair, waves, shape, first)
                chosen = jnp.where(odd, product[rows // 2 :], product[0 : rows // 2])
                if which == 0:
                    picked.append(jnp.where(leading, chosen, jnp.roll(chosen, -2, axis=0)))
                else:
                    picked.append(jnp.where(leading, jnp.roll(chosen, 2, axis=0), chosen))
            component = lax.broadcasted_iota(jnp.int32, picked[0].shape, 0) % 4
            out_ref[index, :, first:last] = jnp.where(component < 2, picked[0], picked[1])
        return carry

    lax.fori_loop(0, inner, body, 0)


def analyse(place, z, legendre, steps, levels):
    _, lats, count = legendre.shape
    parts = z.shape[0] // (2 * levels)
    share = lats // parts
    inner = math.gcd(steps, INNER)
    return pl.pallas_call(
        functools.partial(analyse_kernel, levels=levels, parts=parts, share=share, steps=steps),
        grid_spec=pltpu.PrefetchScalarGridSpec(
            num_scalar_prefetch=1,
            grid=(steps // inner,),
            in_specs=[
                pl.BlockSpec(z.shape, lambda i, place: (0, 0, 0)),
                pl.BlockSpec(memory_space=pl.ANY),
            ],
            out_specs=pl.BlockSpec((inner, 4 * levels, count), lambda i, place: (i, 0, 0)),
            scratch_shapes=[
                pltpu.VMEM((DEPTH, 2, lats, count), F32),
                pltpu.SemaphoreType.DMA((DEPTH, 2)),
            ],
        ),
        out_shape=jax.ShapeDtypeStruct((steps, 4 * levels, count), F32),
        compiler_params=params("arbitrary"),
        cost_estimate=cost(16 * 2 * steps * lats * count * WEIGHT, 2 * steps * lats * count * 4),
        name="analyse",
    )(place, z, legendre)


def synthesise_kernel(place_ref, damping_ref, spectrum_ref, legendre_ref, *rest, levels, parts, share, steps):
    out_ref, buffer, sems = rest[-3:]
    inner = spectrum_ref.shape[0]
    count = legendre_ref.shape[2]
    waves = count - 1

    def body(index, carry):
        local_step = pl.program_id(0) * inner + index
        step = place_ref[0] + local_step
        slot = legendre_stream(place_ref, legendre_ref, buffer, sems, local_step, steps)
        target = pl.multiple_of(index * 8, 8)
        totals = [None, None]
        for first, last in ranges(count):
            spectrum = spectrum_ref[index, :, first:last]
            row = lax.broadcasted_iota(jnp.int32, spectrum.shape, 0)
            component = row % 4
            damping = jnp.full(spectrum.shape, damping_ref[levels - 1])
            for v in range(levels - 1):
                damping = jnp.where(row < 4 * (v + 1), damping_ref[v], damping) if v == 0 else damping
            for which in range(2):
                pair = place_ref[1] + 2 * step + which
                column, leading, odd = row_masks(pair, waves, spectrum.shape, first)
                degree = jnp.where(leading, pair + column, column - 1)
                ratio = (degree * (degree + 1)).astype(F32) / float(waves * waves)
                solved = spectrum / (1.0 + damping * ratio)
                if which == 0:
                    doubled = jnp.where(component < 2, solved, jnp.roll(solved, 2, axis=0))
                else:
                    doubled = jnp.where(component < 2, jnp.roll(solved, -2, axis=0), solved)
                keep = jnp.logical_xor(component >= 2, leading)
                north = jnp.where(keep, doubled, 0.0)
                south = jnp.where(odd, -north, north)
                high, low = split(jnp.concatenate([north, south], axis=0))
                both = jnp.concatenate([high, low], axis=0)
                legendre_high, legendre_low = split(buffer[slot, which, :, first:last])
                contract = (((1,), (1,)), ((), ()))
                one = lax.dot_general(legendre_high, both, contract, preferred_element_type=F32)
                two = lax.dot_general(legendre_low, both, contract, preferred_element_type=F32)
                total = one + two
                totals[which] = total if totals[which] is None else totals[which] + total
        rows = 4 * levels * 2
        waves_of = []
        for which in range(2):
            turned = jnp.transpose(totals[which], (1, 0))
            waves_of.append(turned[0:rows] + turned[rows:])
        for hemi in range(2):
            for v in range(levels):
                low = (hemi * levels + v) * 4
                block = jnp.concatenate([w[low : low + 4] for w in waves_of], axis=0)
                for part in range(parts):
                    out_ref[(hemi * levels + v) * parts + part, pl.ds(target, 8), 0:share] = block[:, part * share : (part + 1) * share]
        return carry

    lax.fori_loop(0, inner, body, 0)


def synthesise(place, damping, spectrum, legendre, previous, sectors, rows):
    _, lats, count = legendre.shape
    levels = damping.shape[0]
    steps = spectrum.shape[0]
    parts = sectors // (2 * levels)
    share = lats // parts
    inner = math.gcd(steps, INNER)
    arguments = [place, damping, spectrum, legendre]
    in_specs = [
        pl.BlockSpec(memory_space=pltpu.SMEM),
        pl.BlockSpec((inner, 4 * levels, count), lambda i, place: (i, 0, 0)),
        pl.BlockSpec(memory_space=pl.ANY),
    ]
    aliases = {}
    if previous is not None:
        arguments.append(previous)
        in_specs.append(pl.BlockSpec(memory_space=pl.ANY))
        aliases = {4: 0}
    return pl.pallas_call(
        functools.partial(synthesise_kernel, levels=levels, parts=parts, share=share, steps=steps),
        grid_spec=pltpu.PrefetchScalarGridSpec(
            num_scalar_prefetch=1,
            grid=(steps // inner,),
            in_specs=in_specs,
            out_specs=pl.BlockSpec((sectors, 8 * inner, LANES), lambda i, place: (0, place[3] + i, 0)),
            scratch_shapes=[
                pltpu.VMEM((DEPTH, 2, lats, count), F32),
                pltpu.SemaphoreType.DMA((DEPTH, 2)),
            ],
        ),
        out_shape=jax.ShapeDtypeStruct((sectors, rows, LANES), F32),
        input_output_aliases=aliases,
        compiler_params=params("arbitrary"),
        cost_estimate=cost(16 * 2 * steps * lats * count * WEIGHT, 2 * steps * lats * count * 4),
        name="synthesise",
    )(*arguments)


def after(value, earlier):
    return value if earlier is None else lax.optimization_barrier((value, earlier))[0]


def exchange(x, sectors):
    return lax.all_to_all(x.reshape(sectors, -1, LANES), "sector", split_axis=0, concat_axis=0, tiled=True)


def solve(fourier, legendre, damping, sectors):
    pairs = legendre.shape[0]
    bands = lax.axis_size("band")
    levels = damping.shape[0]
    bit = lax.axis_index("band") % 2
    pair_start = lax.axis_index("sector") * pairs
    chunks = math.gcd(pairs // 4, CHUNKS)
    each = chunks // SPLITS
    steps = pairs // (2 * 2 * chunks)
    half = pairs // 4
    blocks = steps // math.gcd(steps, INNER)
    rows = 4 * pairs // SPLITS

    def place(side, chunk):
        inside = side * each + chunk % each
        return jnp.stack([side * half + chunk * steps, pair_start, inside * steps, inside * blocks]).astype(jnp.int32)

    def swap(x, mask):
        return lax.ppermute(x, "band", [(i, i ^ mask) for i in range(bands)])

    masks = [1 << n for n in range(1, bands.bit_length()) if 1 << n < bands]
    sums, arrived, z, kept = [], [], None, None
    for c in range(chunks):
        if c % each == 0:
            z = exchange(after(fourier[c // each], z), sectors)
        spot = after(place(1 - bit, c), kept)
        away = analyse(after(spot, sums[c - 2] if c >= 2 else None), z, legendre, steps, levels)
        kept = analyse(after(place(bit, c), away), z, legendre, steps, levels)
        sums.append(kept + swap(away, 1))
        arrived.append(swap(sums[c], masks[0]) if masks else jnp.zeros_like(kept))

    def finished(c, gate):
        total = sums[c] + after(arrived[c], gate)
        for mask in masks[1:]:
            total = total + swap(total, mask)
        return total, swap(total, 1)

    results, result = [], None
    total, other = finished(0, kept)
    for c in range(chunks):
        fresh = c % each == 0
        spot = after(place(bit, c), result) if fresh else place(bit, c)
        result = synthesise(spot, damping, total, legendre, None if fresh else result, sectors, rows)
        mine = other
        if c + 1 < chunks:
            total, other = finished(c + 1, result)
        result = synthesise(place(1 - bit, c), damping, mine, legendre, result, sectors, rows)
        if (c + 1) % each == 0:
            results.append(exchange(result, sectors))
    return results


def local(field, depart, interp_weight, legendre, damping):
    sectors = lax.axis_size("sector")
    hemis, lats, levels, local_lon = field.shape
    pairs = legendre.shape[0]
    lon_count = sectors * local_lon
    radix = math.gcd(RADIX, pairs)
    matrix, twiddle = fourier_tables(lon_count, radix)
    twiddle = jnp.broadcast_to(jnp.asarray(twiddle)[..., None], twiddle.shape + (LANES,))
    forward_tables = split_np(matrix / lon_count) + (twiddle,)
    inverse_tables = split_np(2.0 * matrix.T) + (twiddle,)
    sizes = dict(radix=radix, rows=lon_count, sectors=sectors)
    chunks = (lon_count // SPLITS,) * SPLITS

    advected, packed, share = advect(field, depart, interp_weight, sectors)
    columns = exchange(advected, sectors).reshape(-1, LANES)
    scratch = (lon_count, lon_count) if packed else (lon_count,)
    fourier = transform(forward_kernel, [columns], forward_tables, chunks, scratch, share=share, **sizes)
    returned = solve(fourier, legendre, damping, sectors)
    returned = [x.reshape(-1, LANES) for x in returned]
    final_rows = packed_rows(lon_count, share) if packed else lon_count
    gridded = transform(inverse_kernel, returned, inverse_tables, (final_rows,), scratch, share=share, **sizes)
    final = exchange(gridded[0], sectors)
    if packed:
        return finish(final, hemis, lats, levels, local_lon, share)
    parts = sectors // (hemis * levels)
    final = final[:, :, :share].reshape(hemis, levels, parts, local_lon, share)
    return jnp.transpose(final, (0, 2, 4, 1, 3)).reshape(hemis, lats, levels, local_lon)


def solution(mesh):
    return jax.shard_map(
        local,
        mesh=mesh,
        in_specs=(
            P(None, "band", None, "sector"),
            P(None, "band", "sector"),
            P(None, "band", "sector", None, None),
            P("sector", "band", None),
            P(),
        ),
        out_specs=P(None, "band", None, "sector"),
        check_vma=False,
    )
```

time: 246 us -> 230 us (0.935)
  blocking collectives: 65.8 us -> 45.4 us
  starting transfers between devices: 18 us -> 29 us
  Pallas kernels: 124 us -> 118 us
    all_to_all x3, blocking collectives: 65.8 us -> 45.4 us  [exchange(): lax.all_to_all(x.reshape(sectors, -1, LANES), 'sector', split_axis=0, con...]
    ppermute x6 -> x12, waiting for transfers between devices: 4.15 us -> 18.5 us  [swap(): return lax.ppermute(x, 'band', [(i, i ^ mask) for i in range(bands)])]
    pallas_call x4 -> x8, Pallas kernels: 45.5 us -> 37.4 us  [analyse(): pl.pallas_call(functools.partial(analyse_kernel, levels=levels, parts=par...]
    ppermute x1, waiting for transfers between devices: 9 us -> 1.21 us  [advect(): lax.ppermute(turned[:, :, local - REACH_BACK * width:], 'sector', up)]
    all_to_all x1 -> x3, starting transfers between devices: 3.57 us -> 10.9 us  [exchange(): lax.all_to_all(x.reshape(sectors, -1, LANES), 'sector', split_axis=0, con...]
    all_to_all x1 -> x3, waiting for transfers between devices: 18 us -> 11 us  [exchange(): lax.all_to_all(x.reshape(sectors, -1, LANES), 'sector', split_axis=0, con...]
    ppermute x6 -> x12, starting transfers between devices: 10.9 us -> 14.6 us  [swap(): return lax.ppermute(x, 'band', [(i, i ^ mask) for i in range(bands)])]
    pallas_call x3 -> x5, Pallas kernels: 25 us -> 27 us  [the longest x2 14.9 us: call(): pl.pallas_call(functools.partial(advect_kernel, width=width, parts=parts,...]
  transfers between devices with their start and end apart: 9 -> 17, of which waited for: 3 -> 5; matrix products, arithmetic and copies ran while one was open for 0% -> 1% of each run, Pallas kernels for 26% -> 42%
where the time goes in v2:
time: 230 us
  Pallas kernels  118 us (51%)
  blocking collectives  45.4 us (20%)
  waiting for transfers between devices  30.7 us (13%)
  starting transfers between devices  29 us (13%)
  local copies, waits for them, and re-layouts  5.52 us (2%)
    pallas_call x8, Pallas kernels, synthesise(): pl.pallas_call(functools.partial(synthesise_kernel, levels=levels, parts=...  53.5 us
    all_to_all x3, blocking collectives, exchange(): lax.all_to_all(x.reshape(sectors, -1, LANES), 'sector', split_axis=0, con...  45.4 us
    pallas_call x8, Pallas kernels, analyse(): pl.pallas_call(functools.partial(analyse_kernel, levels=levels, parts=par...  37.4 us
    ppermute x12, waiting for transfers between devices, swap(): return lax.ppermute(x, 'band', [(i, i ^ mask) for i in range(bands)])  18.5 us
    pallas_call x2, Pallas kernels, call(): pl.pallas_call(functools.partial(advect_kernel, width=width, parts=parts,...  14.9 us
    ppermute x12, starting transfers between devices, swap(): return lax.ppermute(x, 'band', [(i, i ^ mask) for i in range(bands)])  14.6 us
    all_to_all x3, waiting for transfers between devices, exchange(): lax.all_to_all(x.reshape(sectors, -1, LANES), 'sector', split_axis=0, con...  11 us
    all_to_all x3, starting transfers between devices, exchange(): lax.all_to_all(x.reshape(sectors, -1, LANES), 'sector', split_axis=0, con...  10.9 us
  transfers between devices with their start and end apart: 17, of which 5 were waited for; matrix products, arithmetic and copies ran while one was open for 1% of the time, Pallas kernels for 42%

profile of v2, /device:TPU:0, one launch (start us, length us, event | category | flops | bytes accessed | tf_op | source)
XLA Modules:
  0.0 229.7 jit_solution(11194007117625384629)
XLA Ops:
  6.5 6.4 %advect_inner.1.refs_5_ = f32[8,200,128]{2,1,0:T(8,128)S(1)} custom-call(s32[2]{0:T(128)S(1)} %copy-done.12, f32[2,2,320,160]{3,2,1,0:T(8,128)S(1)} %bitcast.30, s32[2,10,1,160]{3,2,1,0:T(1,128)S(1)} %copy.24.refs_1_.refs_3_, bf16[2,10,64,32,160]{4,3,2,1,0:T(8,128)(2,1)} %bitcast.36), custom_call_target="tpu_custom_call" | custom-call | flops 83886080 | bytes 7864320 | tf_op jit(solution)/shard_map/advect_inner/pallas_call | solution.py:202
  14.2 8.5 %advect_edge.1 = f32[8,200,128]{2,1,0:T(8,128)S(1)} custom-call(s32[3]{0:T(128)S(1)} %copy-done.11, f32[2,2,320,160]{3,2,1,0:T(8,128)S(1)} %bitcast.31, f32[2,2,64,160]{3,2,1,0:T(8,128)S(1)} %collective-permute-done.refs_1_, f32[2,2,96,160]{3,2,1,0:T(8,128)S(1)} %collective-permute-done.1.refs_2_, ...), custom_call_target="tpu_custom_call", output_to_operand_aliasing={{}: (6, {})} | custom-call | flops 125829120 | bytes 11796480 | tf_op jit(solution)/shard_map/advect_edge/pallas_call | solution.py:202
  22.7 15.4 %all_to_all.30 = f32[8,200,128]{2,1,0:T(8,128)S(1)} all-to-all(f32[8,200,128]{2,1,0:T(8,128)S(1)} %advect_edge.1), channel_id=1, replica_groups=mesh['band'=4,'sector'=8] {'sector'}, dimensions={0} | all-to-all | bytes 1638400 | tf_op jit(solution)/shard_map/all_to_all | solution.py:611
  47.6 10.9 %all-to-all-done.1.z_ref = f32[8,160,128]{2,1,0:T(8,128)S(1)} async-done(((f32[8,160,128]{2,1,0:T(8,128)}), f32[8,160,128]{2,1,0:T(8,128)S(1)}, u32[]{:S(2)}, u32[]{:S(2)}) %all-to-all-start.1) | async-done | bytes 655392 | tf_op jit(solution)/shard_map/all_to_all | solution.py:611
  62.2 4.7 %analyse.8 = f32[5,8,1281]{2,1,0:T(8,128)S(1)} custom-call(s32[4]{0:T(128)S(1)} %add_add_fusion.3.place_ref, f32[8,160,128]{2,1,0:T(8,128)S(1)} %all-to-all-done.1.z_ref, f32[80,160,1281]{2,1,0:T(8,128)} %legendre_ref.31), custom_call_target="tpu_custom_call" | custom-call | flops 65587200 | bytes 8198400 | tf_op jit(solution)/shard_map/analyse/pallas_call | solution.py:490
  68.5 4.7 %analyse.9 = f32[5,8,1281]{2,1,0:T(8,128)S(1)} custom-call(s32[4]{0:T(128)S(1)} %get-tuple-element.23.place_ref, f32[8,160,128]{2,1,0:T(8,128)S(1)} %all-to-all-done.1.z_ref, f32[80,160,1281]{2,1,0:T(8,128)} %legendre_ref.31), custom_call_target="tpu_custom_call" | custom-call | flops 65587200 | bytes 8198400 | tf_op jit(solution)/shard_map/analyse/pallas_call | solution.py:490
  73.2 4.7 %analyse.10 = f32[5,8,1281]{2,1,0:T(8,128)S(1)} custom-call(s32[4]{0:T(128)S(1)} %get-tuple-element.24.place_ref, f32[8,160,128]{2,1,0:T(8,128)S(1)} %all-to-all-done.1.z_ref, f32[80,160,1281]{2,1,0:T(8,128)} %legendre_ref.31), custom_call_target="tpu_custom_call" | custom-call | flops 65587200 | bytes 8198400 | tf_op jit(solution)/shard_map/analyse/pallas_call | solution.py:490
  78.6 4.7 %analyse.11 = f32[5,8,1281]{2,1,0:T(8,128)S(1)} custom-call(s32[4]{0:T(128)S(1)} %add_add_fusion.1.place_ref, f32[8,160,128]{2,1,0:T(8,128)S(1)} %all-to-all-done.1.z_ref, f32[80,160,1281]{2,1,0:T(8,128)} %legendre_ref.31), custom_call_target="tpu_custom_call" | custom-call | flops 65587200 | bytes 8198400 | tf_op jit(solution)/shard_map/analyse/pallas_call | solution.py:490
  88.8 4.7 %analyse.12 = f32[5,8,1281]{2,1,0:T(8,128)S(1)} custom-call(s32[4]{0:T(128)S(1)} %add_add_fusion.7.place_ref, f32[8,160,128]{2,1,0:T(8,128)S(1)} %all-to-all-done.2.z_ref, f32[80,160,1281]{2,1,0:T(8,128)} %legendre_ref.31), custom_call_target="tpu_custom_call" | custom-call | flops 65587200 | bytes 8198400 | tf_op jit(solution)/shard_map/analyse/pallas_call | solution.py:490
  93.5 4.7 %analyse.13 = f32[5,8,1281]{2,1,0:T(8,128)S(1)} custom-call(s32[4]{0:T(128)S(1)} %get-tuple-element.36.place_ref, f32[8,160,128]{2,1,0:T(8,128)S(1)} %all-to-all-done.2.z_ref, f32[80,160,1281]{2,1,0:T(8,128)} %legendre_ref.31), custom_call_target="tpu_custom_call" | custom-call | flops 65587200 | bytes 8198400 | tf_op jit(solution)/shard_map/analyse/pallas_call | solution.py:490
  98.2 4.7 %analyse.14 = f32[5,8,1281]{2,1,0:T(8,128)S(1)} custom-call(s32[4]{0:T(128)S(1)} %get-tuple-element.32.place_ref, f32[8,160,128]{2,1,0:T(8,128)S(1)} %all-to-all-done.2.z_ref, f32[80,160,1281]{2,1,0:T(8,128)} %legendre_ref.31), custom_call_target="tpu_custom_call" | custom-call | flops 65587200 | bytes 8198400 | tf_op jit(solution)/shard_map/analyse/pallas_call | solution.py:490
  102.9 4.7 %analyse.15 = f32[5,8,1281]{2,1,0:T(8,128)S(1)} custom-call(s32[4]{0:T(128)S(1)} %add_add_fusion.4.place_ref, f32[8,160,128]{2,1,0:T(8,128)S(1)} %all-to-all-done.2.z_ref, f32[80,160,1281]{2,1,0:T(8,128)} %legendre_ref.31), custom_call_target="tpu_custom_call" | custom-call | flops 65587200 | bytes 8198400 | tf_op jit(solution)/shard_map/analyse/pallas_call | solution.py:490
  108.1 6.6 %synthesise.8.rest_0_ = f32[8,160,128]{2,1,0:T(8,128)S(1)} custom-call(s32[4]{0:T(128)S(1)} %get-tuple-element.23.place_ref, f32[2]{0:T(128)S(1)} %copy-done.2, f32[5,8,1281]{2,1,0:T(8,128)S(1)} %add.75.spectrum_ref, f32[80,160,1281]{2,1,0:T(8,128)} %legendre_ref.31), custom_call_target="tpu_custom_call" | custom-call | flops 65587200 | bytes 8198400 | tf_op jit(solution)/shard_map/synthesise/pallas_call | solution.py:586
  118.5 6.6 %synthesise.9.rest_0_ = f32[8,160,128]{2,1,0:T(8,128)S(1)} custom-call(s32[4]{0:T(128)S(1)} %copy-done.10, f32[2]{0:T(128)S(1)} %copy-done.2, f32[5,8,1281]{2,1,0:T(8,128)S(1)} %collective-permute-done.7.spectrum_ref, f32[80,160,1281]{2,1,0:T(8,128)} %legendre_ref.31, f32[8,160,128]{2,1,0:T(8,128)S(1)} %synthesise.8.rest_0_), custom_call_target="tpu_custom_call", output_to_operand_aliasing={{}: (4, {})} | custom-call | flops 65587200 | bytes 8198400 | tf_op jit(solution)/shard_map/synthesise/pallas_call | solution.py:586
  125.1 6.6 %synthesise.10 = f32[8,160,128]{2,1,0:T(8,128)S(1)} custom-call(s32[4]{0:T(128)S(1)} %add_add_fusion.1.place_ref, f32[2]{0:T(128)S(1)} %copy-done.2, f32[5,8,1281]{2,1,0:T(8,128)S(1)} %add.76.spectrum_ref, f32[80,160,1281]{2,1,0:T(8,128)} %legendre_ref.31, f32[8,160,128]{2,1,0:T(8,128)S(1)} %synthesise.9.rest_0_), custom_call_target="tpu_custom_call", output_to_operand_aliasing={{}: (4, {})} | custom-call | flops 65587200 | bytes 8198400 | tf_op jit(solution)/shard_map/synthesise/pallas_call | solution.py:586
  132.6 7.3 %synthesise.11 = f32[8,160,128]{2,1,0:T(8,128)} custom-call(s32[4]{0:T(128)S(1)} %copy-done.6, f32[2]{0:T(128)S(1)} %copy-done.2, f32[5,8,1281]{2,1,0:T(8,128)S(1)} %collective-permute-done.6.spectrum_ref, f32[80,160,1281]{2,1,0:T(8,128)} %legendre_ref.31, f32[8,160,128]{2,1,0:T(8,128)} %copy.28.rest_0_), custom_call_target="tpu_custom_call", output_to_operand_aliasing={{}: (4, {})} | custom-call | flops 65587200 | bytes 8198400 | tf_op jit(solution)/shard_map/synthesise/pallas_call | solution.py:586
  146.8 15.4 %collective-permute-done.11 = f32[5,8,1281]{2,1,0:T(8,128)S(1)} collective-permute-done((f32[5,8,1281]{2,1,0:T(8,128)S(1)}, f32[5,8,1281]{2,1,0:T(8,128)S(1)}, u32[]{:S(2)}, u32[]{:S(2)}) %collective-permute-start.11) | collective-permute-done | bytes 204992 | tf_op jit(solution)/shard_map/ppermute | solution.py:632
  162.5 6.6 %synthesise.12.rest_0_ = f32[8,160,128]{2,1,0:T(8,128)S(1)} custom-call(s32[4]{0:T(128)S(1)} %get-tuple-element.36.place_ref, f32[2]{0:T(128)S(1)} %copy-done.2, f32[5,8,1281]{2,1,0:T(8,128)S(1)} %add.79.spectrum_ref, f32[80,160,1281]{2,1,0:T(8,128)} %legendre_ref.31), custom_call_target="tpu_custom_call" | custom-call | flops 65587200 | bytes 8198400 | tf_op jit(solution)/shard_map/synthesise/pallas_call | solution.py:586
  171.9 6.6 %synthesise.13.rest_0_ = f32[8,160,128]{2,1,0:T(8,128)S(1)} custom-call(s32[4]{0:T(128)S(1)} %copy-done.4, f32[2]{0:T(128)S(1)} %copy-done.2, f32[5,8,1281]{2,1,0:T(8,128)S(1)} %collective-permute-done.13.spectrum_ref, f32[80,160,1281]{2,1,0:T(8,128)} %legendre_ref.31, f32[8,160,128]{2,1,0:T(8,128)S(1)} %synthesise.12.rest_0_), custom_call_target="tpu_custom_call", output_to_operand_aliasing={{}: (4, {})} | custom-call | flops 65587200 | bytes 8198400 | tf_op jit(solution)/shard_map/synthesise/pallas_call | solution.py:586
  178.5 6.6 %synthesise.14.rest_0_ = f32[8,160,128]{2,1,0:T(8,128)S(1)} custom-call(s32[4]{0:T(128)S(1)} %add_add_fusion.4.place_ref, f32[2]{0:T(128)S(1)} %copy-done.2, f32[5,8,1281]{2,1,0:T(8,128)S(1)} %add.80.spectrum_ref, f32[80,160,1281]{2,1,0:T(8,128)} %legendre_ref.31, f32[8,160,128]{2,1,0:T(8,128)S(1)} %synthesise.13.rest_0_), custom_call_target="tpu_custom_call", output_to_operand_aliasing={{}: (4, {})} | custom-call | flops 65587200 | bytes 8198400 | tf_op jit(solution)/shard_map/synthesise/pallas_call | solution.py:586
  185.2 6.6 %synthesise.15 = f32[8,160,128]{2,1,0:T(8,128)S(1)} custom-call(s32[4]{0:T(128)S(1)} %copy-done.8, f32[2]{0:T(128)S(1)} %copy-done.2, f32[5,8,1281]{2,1,0:T(8,128)S(1)} %collective-permute-done.12.spectrum_ref, f32[80,160,1281]{2,1,0:T(8,128)} %legendre_ref.31, f32[8,160,128]{2,1,0:T(8,128)S(1)} %synthesise.14.rest_0_), custom_call_target="tpu_custom_call", output_to_operand_aliasing={{}: (4, {})} | custom-call | flops 65587200 | bytes 8198400 | tf_op jit(solution)/shard_map/synthesise/pallas_call | solution.py:586
  191.8 14.7 %all_to_all.31 = f32[8,160,128]{2,1,0:T(8,128)S(1)} all-to-all(f32[8,160,128]{2,1,0:T(8,128)S(1)} %synthesise.15), channel_id=1, replica_groups=mesh['band'=4,'sector'=8] {'sector'}, dimensions={0} | all-to-all | bytes 1310720 | tf_op jit(solution)/shard_map/all_to_all | solution.py:611
  209.1 15.3 %all_to_all.32.x_ref = f32[8,200,128]{2,1,0:T(8,128)S(1)} all-to-all(f32[8,200,128]{2,1,0:T(8,128)S(1)} %bitcast.33), channel_id=1, replica_groups=mesh['band'=4,'sector'=8] {'sector'}, dimensions={0} | all-to-all | bytes 1638400 | tf_op jit(solution)/shard_map/all_to_all | solution.py:611
  224.4 5.3 %finish.1 = f32[2,160,2,320]{3,2,1,0:T(2,128)} custom-call(f32[8,200,128]{2,1,0:T(8,128)S(1)} %all_to_all.32.x_ref), custom_call_target="tpu_custom_call" | custom-call | tf_op jit(solution)/shard_map/finish/pallas_call | solution.py:388
  (90 shorter events, 46.4 us)
Async XLA Ops:
  1.6 12.5 %collective-permute-start.1 = (f32[2,2,96,160]{3,2,1,0:T(8,128)S(1)}, f32[2,2,96,160]{3,2,1,0:T(8,128)S(1)}, u32[]{:S(2)}, u32[]{:S(2)}) collective-permute-start(f32[2,2,96,160]{3,2,1,0:T(8,128)S(1)} %slice.9), channel_id=1, source_target_pairs={{1,0},{2,1},{3,2},{4,3},{5,4},{6,5},{7,6},{0,7},{9,8},{10,9},{11,1... | collective-permute-start | bytes 737288 | tf_op jit(solution)/shard_map/ppermute | solution.py:177
  5.1 9.1 %collective-permute-start = (f32[2,2,64,160]{3,2,1,0:T(8,128)S(1)}, f32[2,2,64,160]{3,2,1,0:T(8,128)S(1)}, u32[]{:S(2)}, u32[]{:S(2)}) collective-permute-start(f32[2,2,64,160]{3,2,1,0:T(8,128)S(1)} %slice.8), channel_id=1, source_target_pairs={{0,1},{1,2},{2,3},{3,4},{4,5},{5,6},{6,7},{7,0},{8,9},{9,10},{10,1... | collective-permute-start | bytes 491528 | tf_op jit(solution)/shard_map/ppermute | solution.py:176
  6.5 31.6 %copy-start.17 = (f32[9,2,160]{2,1,0:T(2,128)S(1)}, f32[9,2,160]{2,1,0:T(2,128)}, u32[]{:S(2)}) copy-start(f32[9,2,160]{2,1,0:T(2,128)} %constant.48.clone) | copy-start | bytes 34564
  6.5 32.0 %copy-start.15 = (bf16[320,320]{1,0:T(8,128)(2,1)S(1)}, bf16[320,320]{1,0:T(8,128)(2,1)}, u32[]{:S(2)}) copy-start(bf16[320,320]{1,0:T(8,128)(2,1)} %constant.52.clone.low_ref) | copy-start | bytes 614404
  6.5 32.0 %copy-start.16 = (bf16[320,320]{1,0:T(8,128)(2,1)S(1)}, bf16[320,320]{1,0:T(8,128)(2,1)}, u32[]{:S(2)}) copy-start(bf16[320,320]{1,0:T(8,128)(2,1)} %constant.51.clone.high_ref) | copy-start | bytes 614404
  44.0 14.6 %all-to-all-start.1 = ((f32[8,160,128]{2,1,0:T(8,128)}), f32[8,160,128]{2,1,0:T(8,128)S(1)}, u32[]{:S(2)}, u32[]{:S(2)}) async-start(f32[8,160,128]{2,1,0:T(8,128)} %bitcast.18), calls=%async_computation.1 | async-start | bytes 1310720 | tf_op jit(solution)/shard_map/all_to_all | solution.py:611
  47.6 25.6 %copy-start.5 = (s32[4]{0:T(128)}, s32[4]{0:T(128)S(1)}, u32[]{:S(2)}) copy-start(s32[4]{0:T(128)S(1)} %get-tuple-element.24.place_ref) | copy-start | bytes 52
  58.6 30.2 %all-to-all-start.2 = ((f32[8,160,128]{2,1,0:T(8,128)}), f32[8,160,128]{2,1,0:T(8,128)S(1)}, u32[]{:S(2)}, u32[]{:S(2)}) async-start(f32[8,160,128]{2,1,0:T(8,128)} %bitcast.23), calls=%async_computation.2 | async-start | bytes 1310720 | tf_op jit(solution)/shard_map/all_to_all | solution.py:611
  66.9 21.3 %collective-permute-start.4 = (f32[5,8,1281]{2,1,0:T(8,128)S(1)}, f32[5,8,1281]{2,1,0:T(8,128)S(1)}, u32[]{:S(2)}, u32[]{:S(2)}) collective-permute-start(f32[5,8,1281]{2,1,0:T(8,128)S(1)} %analyse.8), channel_id=1, source_target_pairs={{0,8},{8,0},{16,24},{24,16},{1,9},{9,1},{17,25},{25,17},{2,10},{10... | collective-permute-start | bytes 614888 | tf_op jit(solution)/shard_map/ppermute | solution.py:632
  77.9 7.6 %collective-permute-start.2 = (f32[5,8,1281]{2,1,0:T(8,128)S(1)}, f32[5,8,1281]{2,1,0:T(8,128)S(1)}, u32[]{:S(2)}, u32[]{:S(2)}) collective-permute-start(f32[5,8,1281]{2,1,0:T(8,128)S(1)} %analyse.10), channel_id=1, source_target_pairs={{0,8},{8,0},{16,24},{24,16},{1,9},{9,1},{17,25},{25,17},{2,10},{10... | collective-permute-start | bytes 614888 | tf_op jit(solution)/shard_map/ppermute | solution.py:632
  85.5 29.2 %collective-permute-start.3 = (f32[5,8,1281]{2,1,0:T(8,128)S(1)}, f32[5,8,1281]{2,1,0:T(8,128)S(1)}, u32[]{:S(2)}, u32[]{:S(2)}) collective-permute-start(f32[5,8,1281]{2,1,0:T(8,128)S(1)} %add.69), channel_id=1, source_target_pairs={{0,16},{8,24},{16,0},{24,8},{1,17},{9,25},{17,1},{25,9},{2,18},{10... | collective-permute-start | bytes 614888 | tf_op jit(solution)/shard_map/ppermute | solution.py:632
  88.2 19.3 %collective-permute-start.5 = (f32[5,8,1281]{2,1,0:T(8,128)S(1)}, f32[5,8,1281]{2,1,0:T(8,128)S(1)}, u32[]{:S(2)}, u32[]{:S(2)}) collective-permute-start(f32[5,8,1281]{2,1,0:T(8,128)S(1)} %add.70), channel_id=1, source_target_pairs={{0,16},{8,24},{16,0},{24,8},{1,17},{9,25},{17,1},{25,9},{2,18},{10... | collective-permute-start | bytes 614888 | tf_op jit(solution)/shard_map/ppermute | solution.py:632
  107.6 10.8 %collective-permute-start.7 = (f32[5,8,1281]{2,1,0:T(8,128)S(1)}, f32[5,8,1281]{2,1,0:T(8,128)S(1)}, u32[]{:S(2)}, u32[]{:S(2)}) collective-permute-start(f32[5,8,1281]{2,1,0:T(8,128)S(1)} %add.75.spectrum_ref), channel_id=1, source_target_pairs={{0,8},{8,0},{16,24},{24,16},{1,9},{9,1},{17,25},{25,17},{2,10},{10... | collective-permute-start | bytes 614888 | tf_op jit(solution)/shard_map/ppermute | solution.py:632
  114.8 17.7 %collective-permute-start.6 = (f32[5,8,1281]{2,1,0:T(8,128)S(1)}, f32[5,8,1281]{2,1,0:T(8,128)S(1)}, u32[]{:S(2)}, u32[]{:S(2)}) collective-permute-start(f32[5,8,1281]{2,1,0:T(8,128)S(1)} %add.76.spectrum_ref), channel_id=1, source_target_pairs={{0,8},{8,0},{16,24},{24,16},{1,9},{9,1},{17,25},{25,17},{2,10},{10... | collective-permute-start | bytes 614888 | tf_op jit(solution)/shard_map/ppermute | solution.py:632
  116.4 27.2 %collective-permute-start.10 = (f32[5,8,1281]{2,1,0:T(8,128)S(1)}, f32[5,8,1281]{2,1,0:T(8,128)S(1)}, u32[]{:S(2)}, u32[]{:S(2)}) collective-permute-start(f32[5,8,1281]{2,1,0:T(8,128)S(1)} %analyse.12), channel_id=1, source_target_pairs={{0,8},{8,0},{16,24},{24,16},{1,9},{9,1},{17,25},{25,17},{2,10},{10... | collective-permute-start | bytes 614888 | tf_op jit(solution)/shard_map/ppermute | solution.py:632
  116.9 29.5 %collective-permute-start.8 = (f32[5,8,1281]{2,1,0:T(8,128)S(1)}, f32[5,8,1281]{2,1,0:T(8,128)S(1)}, u32[]{:S(2)}, u32[]{:S(2)}) collective-permute-start(f32[5,8,1281]{2,1,0:T(8,128)S(1)} %analyse.14), channel_id=1, source_target_pairs={{0,8},{8,0},{16,24},{24,16},{1,9},{9,1},{17,25},{25,17},{2,10},{10... | collective-permute-start | bytes 614888 | tf_op jit(solution)/shard_map/ppermute | solution.py:632
  139.8 52.0 %all-to-all-start.3 = ((f32[8,160,128]{2,1,0:T(8,128)}), f32[8,160,128]{2,1,0:T(8,128)S(1)}, u32[]{:S(2)}, u32[]{:S(2)}) async-start(f32[8,160,128]{2,1,0:T(8,128)} %synthesise.11), calls=%async_computation.3 | async-start | bytes 1310720 | tf_op jit(solution)/shard_map/all_to_all | solution.py:611
  143.7 18.5 %collective-permute-start.11 = (f32[5,8,1281]{2,1,0:T(8,128)S(1)}, f32[5,8,1281]{2,1,0:T(8,128)S(1)}, u32[]{:S(2)}, u32[]{:S(2)}) collective-permute-start(f32[5,8,1281]{2,1,0:T(8,128)S(1)} %add.78), channel_id=1, source_target_pairs={{0,16},{8,24},{16,0},{24,8},{1,17},{9,25},{17,1},{25,9},{2,18},{10... | collective-permute-start | bytes 614888 | tf_op jit(solution)/shard_map/ppermute | solution.py:632
  146.4 22.7 %collective-permute-start.9 = (f32[5,8,1281]{2,1,0:T(8,128)S(1)}, f32[5,8,1281]{2,1,0:T(8,128)S(1)}, u32[]{:S(2)}, u32[]{:S(2)}) collective-permute-start(f32[5,8,1281]{2,1,0:T(8,128)S(1)} %add.77), channel_id=1, source_target_pairs={{0,16},{8,24},{16,0},{24,8},{1,17},{9,25},{17,1},{25,9},{2,18},{10... | collective-permute-start | bytes 614888 | tf_op jit(solution)/shard_map/ppermute | solution.py:632
  162.2 9.7 %collective-permute-start.13 = (f32[5,8,1281]{2,1,0:T(8,128)S(1)}, f32[5,8,1281]{2,1,0:T(8,128)S(1)}, u32[]{:S(2)}, u32[]{:S(2)}) collective-permute-start(f32[5,8,1281]{2,1,0:T(8,128)S(1)} %add.79.spectrum_ref), channel_id=1, source_target_pairs={{0,8},{8,0},{16,24},{24,16},{1,9},{9,1},{17,25},{25,17},{2,10},{10... | collective-permute-start | bytes 614888 | tf_op jit(solution)/shard_map/ppermute | solution.py:632
  169.2 16.0 %collective-permute-start.12 = (f32[5,8,1281]{2,1,0:T(8,128)S(1)}, f32[5,8,1281]{2,1,0:T(8,128)S(1)}, u32[]{:S(2)}, u32[]{:S(2)}) collective-permute-start(f32[5,8,1281]{2,1,0:T(8,128)S(1)} %add.80.spectrum_ref), channel_id=1, source_target_pairs={{0,8},{8,0},{16,24},{24,16},{1,9},{9,1},{17,25},{25,17},{2,10},{10... | collective-permute-start | bytes 614888 | tf_op jit(solution)/shard_map/ppermute | solution.py:632
  185.1 21.4 %copy-start.1 = (f32[9,2,160,128]{3,2,1,0:T(8,128)S(1)}, f32[9,2,160,128]{3,2,1,0:T(8,128)}, u32[]{:S(2)}) copy-start(f32[9,2,160,128]{3,2,1,0:T(8,128)} %copy-done) | copy-start | bytes 4423684
  185.2 21.4 %copy-start.13 = (bf16[320,320]{1,0:T(8,128)(2,1)S(1)}, bf16[320,320]{1,0:T(8,128)(2,1)}, u32[]{:S(2)}) copy-start(bf16[320,320]{1,0:T(8,128)(2,1)} %constant.54.clone.refs_3_) | copy-start | bytes 614404
  185.2 21.4 %copy-start.14 = (bf16[320,320]{1,0:T(8,128)(2,1)S(1)}, bf16[320,320]{1,0:T(8,128)(2,1)}, u32[]{:S(2)}) copy-start(bf16[320,320]{1,0:T(8,128)(2,1)} %constant.53.clone.refs_2_) | copy-start | bytes 614404
  (11 other events, 80.3 us)

commit v3 on v2

--- a/solution.py
+++ b/solution.py
@@ -12,7 +12,7 @@
 
 REACH_BACK = 2
 REACH_AHEAD = 3
-CHUNKS = 4
+CHUNKS = 2
 SPLITS = 2
 INNER = 5
 LANES = 128
@@ -654,10 +654,9 @@
         fresh = c % each == 0
         spot = after(place(bit, c), result) if fresh else place(bit, c)
         result = synthesise(spot, damping, total, legendre, None if fresh else result, sectors, rows)
-        mine = other
+        result = synthesise(place(1 - bit, c), damping, other, legendre, result, sectors, rows)
         if c + 1 < chunks:
             total, other = finished(c + 1, result)
-        result = synthesise(place(1 - bit, c), damping, mine, legendre, result, sectors, rows)
         if (c + 1) % each == 0:
             results.append(exchange(result, sectors))
     return results

time: 230 us -> 206 us (0.90)
  Pallas kernels: 118 us -> 101 us
  waiting for transfers between devices: 30.7 us -> 27.4 us
    pallas_call x8 -> x4, Pallas kernels: 53.5 us -> 43.9 us  [synthesise(): pl.pallas_call(functools.partial(synthesise_kernel, levels=levels, parts=...]
    pallas_call x8 -> x4, Pallas kernels: 37.4 us -> 29.7 us  [analyse(): pl.pallas_call(functools.partial(analyse_kernel, levels=levels, parts=par...]
    ppermute x12 -> x6, waiting for transfers between devices: 18.5 us -> 15.2 us  [swap(): return lax.ppermute(x, 'band', [(i, i ^ mask) for i in range(bands)])]
    ppermute x12 -> x6, starting transfers between devices: 14.6 us -> 12.5 us  [swap(): return lax.ppermute(x, 'band', [(i, i ^ mask) for i in range(bands)])]
  transfers between devices with their start and end apart: 17 -> 11, of which waited for: 5 -> 6; matrix products, arithmetic and copies ran while one was open for 1% -> 1% of each run, Pallas kernels for 42% -> 39%
where the time goes in v3:
time: 206 us
  Pallas kernels  101 us (49%)
  blocking collectives  45.5 us (22%)
  waiting for transfers between devices  27.4 us (13%)
  starting transfers between devices  26.9 us (13%)
  local copies, waits for them, and re-layouts  4.64 us (2%)
    all_to_all x3, blocking collectives, exchange(): lax.all_to_all(x.reshape(sectors, -1, LANES), 'sector', split_axis=0, con...  45.5 us
    pallas_call x4, Pallas kernels, synthesise(): pl.pallas_call(functools.partial(synthesise_kernel, levels=levels, parts=...  43.9 us
    pallas_call x4, Pallas kernels, analyse(): pl.pallas_call(functools.partial(analyse_kernel, levels=levels, parts=par...  29.7 us
    ppermute x6, waiting for transfers between devices, swap(): return lax.ppermute(x, 'band', [(i, i ^ mask) for i in range(bands)])  15.2 us
    pallas_call x2, Pallas kernels, call(): pl.pallas_call(functools.partial(advect_kernel, width=width, parts=parts,...  14.9 us
    ppermute x6, starting transfers between devices, swap(): return lax.ppermute(x, 'band', [(i, i ^ mask) for i in range(bands)])  12.5 us
    all_to_all x3, waiting for transfers between devices, exchange(): lax.all_to_all(x.reshape(sectors, -1, LANES), 'sector', split_axis=0, con...  11 us
    all_to_all x3, starting transfers between devices, exchange(): lax.all_to_all(x.reshape(sectors, -1, LANES), 'sector', split_axis=0, con...  10.9 us
  transfers between devices with their start and end apart: 11, of which 6 were waited for; matrix products, arithmetic and copies ran while one was open for 1% of the time, Pallas kernels for 39%

profile of v3, /device:TPU:0, one launch (start us, length us, event | category | flops | bytes accessed | tf_op | source)
XLA Modules:
  0.0 205.8 jit_solution(1604098920634406192)
XLA Ops:
  1.6 3.4 %collective-permute-start.1 = (f32[2,2,96,160]{3,2,1,0:T(8,128)S(1)}, f32[2,2,96,160]{3,2,1,0:T(8,128)S(1)}, u32[]{:S(2)}, u32[]{:S(2)}) collective-permute-start(f32[2,2,96,160]{3,2,1,0:T(8,128)S(1)} %slice.9), channel_id=1, source_target_pairs={{1,0},{2,1},{3,2},{4,3},{5,4},{6,5},{7,6},{0,7},{9,8},{10,9},{11,1... | collective-permute-start | bytes 737288 | tf_op jit(solution)/shard_map/ppermute | solution.py:177
  6.5 6.4 %advect_inner.1.refs_5_ = f32[8,200,128]{2,1,0:T(8,128)S(1)} custom-call(s32[2]{0:T(128)S(1)} %copy-done.4, f32[2,2,320,160]{3,2,1,0:T(8,128)S(1)} %bitcast.22, s32[2,10,1,160]{3,2,1,0:T(1,128)S(1)} %copy.20.refs_1_.refs_3_, bf16[2,10,64,32,160]{4,3,2,1,0:T(8,128)(2,1)} %bitcast.28), custom_call_target="tpu_custom_call" | custom-call | flops 83886080 | bytes 7864320 | tf_op jit(solution)/shard_map/advect_inner/pallas_call | solution.py:202
  14.2 8.5 %advect_edge.1 = f32[8,200,128]{2,1,0:T(8,128)S(1)} custom-call(s32[3]{0:T(128)S(1)} %copy-done.3, f32[2,2,320,160]{3,2,1,0:T(8,128)S(1)} %bitcast.23, f32[2,2,64,160]{3,2,1,0:T(8,128)S(1)} %collective-permute-done.refs_1_, f32[2,2,96,160]{3,2,1,0:T(8,128)S(1)} %collective-permute-done.1.refs_2_, ...), custom_call_target="tpu_custom_call", output_to_operand_aliasing={{}: (6, {})} | custom-call | flops 125829120 | bytes 11796480 | tf_op jit(solution)/shard_map/advect_edge/pallas_call | solution.py:202
  22.7 15.4 %all_to_all.30 = f32[8,200,128]{2,1,0:T(8,128)S(1)} all-to-all(f32[8,200,128]{2,1,0:T(8,128)S(1)} %advect_edge.1), channel_id=1, replica_groups=mesh['band'=4,'sector'=8] {'sector'}, dimensions={0} | all-to-all | bytes 1638400 | tf_op jit(solution)/shard_map/all_to_all | solution.py:611
  38.6 4.2 %shard_map.118 = (f32[1280,128]{1,0:T(8,128)}, f32[1280,128]{1,0:T(8,128)}) custom-call(f32[1600,128]{1,0:T(8,128)S(1)} %bitcast.24, bf16[320,320]{1,0:T(8,128)(2,1)S(1)} %copy-done.7, bf16[320,320]{1,0:T(8,128)(2,1)S(1)} %copy-done.8, f32[9,2,160,128]{3,2,1,0:T(8,128)S(1)} %broadcast_in_dim.10.twiddle_ref.refs_4_), custom_call_target="tpu_custom_call" | custom-call | flops 1258291200 | bytes 2621440 | tf_op jit(solution)/shard_map/pallas_call | solution.py:403
  44.0 3.5 %all-to-all-start.1 = ((f32[8,160,128]{2,1,0:T(8,128)}), f32[8,160,128]{2,1,0:T(8,128)S(1)}, u32[]{:S(2)}, u32[]{:S(2)}) async-start(f32[8,160,128]{2,1,0:T(8,128)} %bitcast.12), calls=%async_computation.1 | async-start | bytes 1310720 | tf_op jit(solution)/shard_map/all_to_all | solution.py:611
  47.6 11.0 %all-to-all-done.1.z_ref = f32[8,160,128]{2,1,0:T(8,128)S(1)} async-done(((f32[8,160,128]{2,1,0:T(8,128)}), f32[8,160,128]{2,1,0:T(8,128)S(1)}, u32[]{:S(2)}, u32[]{:S(2)}) %all-to-all-start.1) | async-done | bytes 655392 | tf_op jit(solution)/shard_map/all_to_all | solution.py:611
  58.6 3.5 %all-to-all-start.2 = ((f32[8,160,128]{2,1,0:T(8,128)}), f32[8,160,128]{2,1,0:T(8,128)S(1)}, u32[]{:S(2)}, u32[]{:S(2)}) async-start(f32[8,160,128]{2,1,0:T(8,128)} %bitcast.15), calls=%async_computation.2 | async-start | bytes 1310720 | tf_op jit(solution)/shard_map/all_to_all | solution.py:611
  62.1 7.4 %analyse.4 = f32[10,8,1281]{2,1,0:T(8,128)S(1)} custom-call(s32[4]{0:T(128)S(1)} %add_add_fusion.place_ref, f32[8,160,128]{2,1,0:T(8,128)S(1)} %all-to-all-done.1.z_ref, f32[80,160,1281]{2,1,0:T(8,128)} %legendre_ref.15), custom_call_target="tpu_custom_call" | custom-call | flops 131174400 | bytes 16396800 | tf_op jit(solution)/shard_map/analyse/pallas_call | solution.py:490
  71.3 7.4 %analyse.5 = f32[10,8,1281]{2,1,0:T(8,128)S(1)} custom-call(s32[4]{0:T(128)S(1)} %get-tuple-element.15.place_ref, f32[8,160,128]{2,1,0:T(8,128)S(1)} %all-to-all-done.1.z_ref, f32[80,160,1281]{2,1,0:T(8,128)} %legendre_ref.15), custom_call_target="tpu_custom_call" | custom-call | flops 131174400 | bytes 16396800 | tf_op jit(solution)/shard_map/analyse/pallas_call | solution.py:490
  78.7 3.5 %collective-permute-done.2 = f32[10,8,1281]{2,1,0:T(8,128)S(1)} collective-permute-done((f32[10,8,1281]{2,1,0:T(8,128)S(1)}, f32[10,8,1281]{2,1,0:T(8,128)S(1)}, u32[]{:S(2)}, u32[]{:S(2)}) %collective-permute-start.2) | collective-permute-done | bytes 409952 | tf_op jit(solution)/shard_map/ppermute | solution.py:632
  85.0 7.4 %analyse.6 = f32[10,8,1281]{2,1,0:T(8,128)S(1)} custom-call(s32[4]{0:T(128)S(1)} %get-tuple-element.16.place_ref, f32[8,160,128]{2,1,0:T(8,128)S(1)} %all-to-all-done.2.z_ref, f32[80,160,1281]{2,1,0:T(8,128)} %legendre_ref.15), custom_call_target="tpu_custom_call" | custom-call | flops 131174400 | bytes 16396800 | tf_op jit(solution)/shard_map/analyse/pallas_call | solution.py:490
  94.1 7.4 %analyse.7 = f32[10,8,1281]{2,1,0:T(8,128)S(1)} custom-call(s32[4]{0:T(128)S(1)} %add_add_fusion.2.place_ref, f32[8,160,128]{2,1,0:T(8,128)S(1)} %all-to-all-done.2.z_ref, f32[80,160,1281]{2,1,0:T(8,128)} %legendre_ref.15), custom_call_target="tpu_custom_call" | custom-call | flops 131174400 | bytes 16396800 | tf_op jit(solution)/shard_map/analyse/pallas_call | solution.py:490
  101.6 3.3 %collective-permute-done.3 = f32[10,8,1281]{2,1,0:T(8,128)S(1)} collective-permute-done((f32[10,8,1281]{2,1,0:T(8,128)S(1)}, f32[10,8,1281]{2,1,0:T(8,128)S(1)}, u32[]{:S(2)}, u32[]{:S(2)}) %collective-permute-start.3) | collective-permute-done | bytes 409952 | tf_op jit(solution)/shard_map/ppermute | solution.py:632
  105.6 8.1 %collective-permute-done.5 = f32[10,8,1281]{2,1,0:T(8,128)S(1)} collective-permute-done((f32[10,8,1281]{2,1,0:T(8,128)S(1)}, f32[10,8,1281]{2,1,0:T(8,128)S(1)}, u32[]{:S(2)}, u32[]{:S(2)}) %collective-permute-start.5) | collective-permute-done | bytes 409952 | tf_op jit(solution)/shard_map/ppermute | solution.py:632
  114.8 11.3 %synthesise.4.rest_0_ = f32[8,160,128]{2,1,0:T(8,128)} custom-call(s32[4]{0:T(128)S(1)} %get-tuple-element.15.place_ref, f32[2]{0:T(128)S(1)} %copy-done.2, f32[10,8,1281]{2,1,0:T(8,128)S(1)} %add.28.spectrum_ref, f32[80,160,1281]{2,1,0:T(8,128)} %legendre_ref.15), custom_call_target="tpu_custom_call" | custom-call | flops 131174400 | bytes 16396800 | tf_op jit(solution)/shard_map/synthesise/pallas_call | solution.py:586
  126.1 11.3 %synthesise.5 = f32[8,160,128]{2,1,0:T(8,128)} custom-call(s32[4]{0:T(128)S(1)} %add_add_fusion.place_ref, f32[2]{0:T(128)S(1)} %copy-done.2, f32[10,8,1281]{2,1,0:T(8,128)S(1)} %collective-permute-done.4.spectrum_ref, f32[80,160,1281]{2,1,0:T(8,128)} %legendre_ref.15, f32[8,160,128]{2,1,0:T(8,128)} %synthesise.4.rest_0_), custom_call_target="tpu_custom_call", output_to_operand_aliasing={{}: (4, {})} | custom-call | flops 131174400 | bytes 16396800 | tf_op jit(solution)/shard_map/synthesise/pallas_call | solution.py:586
  137.5 3.9 %all-to-all-start.3 = ((f32[8,160,128]{2,1,0:T(8,128)}), f32[8,160,128]{2,1,0:T(8,128)S(1)}, u32[]{:S(2)}, u32[]{:S(2)}) async-start(f32[8,160,128]{2,1,0:T(8,128)} %synthesise.5), calls=%async_computation.3 | async-start | bytes 1310720 | tf_op jit(solution)/shard_map/all_to_all | solution.py:611
  141.4 4.7 %collective-permute-start.7 = (f32[10,8,1281]{2,1,0:T(8,128)S(1)}, f32[10,8,1281]{2,1,0:T(8,128)S(1)}, u32[]{:S(2)}, u32[]{:S(2)}) collective-permute-start(f32[10,8,1281]{2,1,0:T(8,128)S(1)} %add.30.spectrum_ref), channel_id=1, source_target_pairs={{0,8},{8,0},{16,24},{24,16},{1,9},{9,1},{17,25},{25,17},{2,10},{10... | collective-permute-start | bytes 1229768 | tf_op jit(solution)/shard_map/ppermute | solution.py:632
  146.1 10.7 %synthesise.6.rest_0_ = f32[8,160,128]{2,1,0:T(8,128)S(1)} custom-call(s32[4]{0:T(128)S(1)} %add_add_fusion.2.place_ref, f32[2]{0:T(128)S(1)} %copy-done.2, f32[10,8,1281]{2,1,0:T(8,128)S(1)} %add.30.spectrum_ref, f32[80,160,1281]{2,1,0:T(8,128)} %legendre_ref.15), custom_call_target="tpu_custom_call" | custom-call | flops 131174400 | bytes 16396800 | tf_op jit(solution)/shard_map/synthesise/pallas_call | solution.py:586
  157.1 10.7 %synthesise.7 = f32[8,160,128]{2,1,0:T(8,128)S(1)} custom-call(s32[4]{0:T(128)S(1)} %get-tuple-element.16.place_ref, f32[2]{0:T(128)S(1)} %copy-done.2, f32[10,8,1281]{2,1,0:T(8,128)S(1)} %collective-permute-done.7.spectrum_ref, f32[80,160,1281]{2,1,0:T(8,128)} %legendre_ref.15, f32[8,160,128]{2,1,0:T(8,128)S(1)} %synthesise.6.rest_0_), custom_call_target="tpu_custom_call", output_to_operand_aliasing={{}: (4, {})} | custom-call | flops 131174400 | bytes 16396800 | tf_op jit(solution)/shard_map/synthesise/pallas_call | solution.py:586
  167.8 14.8 %all_to_all.31 = f32[8,160,128]{2,1,0:T(8,128)S(1)} all-to-all(f32[8,160,128]{2,1,0:T(8,128)S(1)} %synthesise.7), channel_id=1, replica_groups=mesh['band'=4,'sector'=8] {'sector'}, dimensions={0} | all-to-all | bytes 1310720 | tf_op jit(solution)/shard_map/all_to_all | solution.py:611
  185.2 15.3 %all_to_all.32.x_ref = f32[8,200,128]{2,1,0:T(8,128)S(1)} all-to-all(f32[8,200,128]{2,1,0:T(8,128)S(1)} %bitcast.25), channel_id=1, replica_groups=mesh['band'=4,'sector'=8] {'sector'}, dimensions={0} | all-to-all | bytes 1638400 | tf_op jit(solution)/shard_map/all_to_all | solution.py:611
  200.5 5.3 %finish.1 = f32[2,160,2,320]{3,2,1,0:T(2,128)} custom-call(f32[8,200,128]{2,1,0:T(8,128)S(1)} %all_to_all.32.x_ref), custom_call_target="tpu_custom_call" | custom-call | tf_op jit(solution)/shard_map/finish/pallas_call | solution.py:388
  (46 shorter events, 17.0 us)
Async XLA Ops:
  0.0 14.2 %copy-start.3 = (s32[3]{0:T(128)S(1)}, s32[3]{0:T(128)}, u32[]{:S(2)}) copy-start(s32[3]{0:T(128)} %constant.44.clone.groups_ref) | copy-start | bytes 40
  1.6 12.5 %collective-permute-start.1 = (f32[2,2,96,160]{3,2,1,0:T(8,128)S(1)}, f32[2,2,96,160]{3,2,1,0:T(8,128)S(1)}, u32[]{:S(2)}, u32[]{:S(2)}) collective-permute-start(f32[2,2,96,160]{3,2,1,0:T(8,128)S(1)} %slice.9), channel_id=1, source_target_pairs={{1,0},{2,1},{3,2},{4,3},{5,4},{6,5},{7,6},{0,7},{9,8},{10,9},{11,1... | collective-permute-start | bytes 737288 | tf_op jit(solution)/shard_map/ppermute | solution.py:177
  5.1 9.1 %collective-permute-start = (f32[2,2,64,160]{3,2,1,0:T(8,128)S(1)}, f32[2,2,64,160]{3,2,1,0:T(8,128)S(1)}, u32[]{:S(2)}, u32[]{:S(2)}) collective-permute-start(f32[2,2,64,160]{3,2,1,0:T(8,128)S(1)} %slice.8), channel_id=1, source_target_pairs={{0,1},{1,2},{2,3},{3,4},{4,5},{5,6},{6,7},{7,0},{8,9},{9,10},{10,1... | collective-permute-start | bytes 491528 | tf_op jit(solution)/shard_map/ppermute | solution.py:176
  5.9 0.7 copy-start.4
  6.5 31.6 %copy-start.9 = (f32[9,2,160]{2,1,0:T(2,128)S(1)}, f32[9,2,160]{2,1,0:T(2,128)}, u32[]{:S(2)}) copy-start(f32[9,2,160]{2,1,0:T(2,128)} %constant.42.clone) | copy-start | bytes 34564
  6.5 32.0 %copy-start.7 = (bf16[320,320]{1,0:T(8,128)(2,1)S(1)}, bf16[320,320]{1,0:T(8,128)(2,1)}, u32[]{:S(2)}) copy-start(bf16[320,320]{1,0:T(8,128)(2,1)} %constant.45.clone.high_ref) | copy-start | bytes 614404
  6.5 32.0 %copy-start.8 = (bf16[320,320]{1,0:T(8,128)(2,1)S(1)}, bf16[320,320]{1,0:T(8,128)(2,1)}, u32[]{:S(2)}) copy-start(bf16[320,320]{1,0:T(8,128)(2,1)} %constant.46.clone.low_ref) | copy-start | bytes 614404
  42.8 1.1 copy-start
  44.0 14.6 %all-to-all-start.1 = ((f32[8,160,128]{2,1,0:T(8,128)}), f32[8,160,128]{2,1,0:T(8,128)S(1)}, u32[]{:S(2)}, u32[]{:S(2)}) async-start(f32[8,160,128]{2,1,0:T(8,128)} %bitcast.12), calls=%async_computation.1 | async-start | bytes 1310720 | tf_op jit(solution)/shard_map/all_to_all | solution.py:611
  58.6 26.4 %all-to-all-start.2 = ((f32[8,160,128]{2,1,0:T(8,128)}), f32[8,160,128]{2,1,0:T(8,128)S(1)}, u32[]{:S(2)}, u32[]{:S(2)}) async-start(f32[8,160,128]{2,1,0:T(8,128)} %bitcast.15), calls=%async_computation.2 | async-start | bytes 1310720 | tf_op jit(solution)/shard_map/all_to_all | solution.py:611
  69.6 12.7 %collective-permute-start.2 = (f32[10,8,1281]{2,1,0:T(8,128)S(1)}, f32[10,8,1281]{2,1,0:T(8,128)S(1)}, u32[]{:S(2)}, u32[]{:S(2)}) collective-permute-start(f32[10,8,1281]{2,1,0:T(8,128)S(1)} %analyse.4), channel_id=1, source_target_pairs={{0,8},{8,0},{16,24},{24,16},{1,9},{9,1},{17,25},{25,17},{2,10},{10... | collective-permute-start | bytes 1229768 | tf_op jit(solution)/shard_map/ppermute | solution.py:632
  82.3 22.5 %collective-permute-start.3 = (f32[10,8,1281]{2,1,0:T(8,128)S(1)}, f32[10,8,1281]{2,1,0:T(8,128)S(1)}, u32[]{:S(2)}, u32[]{:S(2)}) collective-permute-start(f32[10,8,1281]{2,1,0:T(8,128)S(1)} %add.25), channel_id=1, source_target_pairs={{0,16},{8,24},{16,0},{24,8},{1,17},{9,25},{17,1},{25,9},{2,18},{10... | collective-permute-start | bytes 1229768 | tf_op jit(solution)/shard_map/ppermute | solution.py:632
  92.4 21.2 %collective-permute-start.5 = (f32[10,8,1281]{2,1,0:T(8,128)S(1)}, f32[10,8,1281]{2,1,0:T(8,128)S(1)}, u32[]{:S(2)}, u32[]{:S(2)}) collective-permute-start(f32[10,8,1281]{2,1,0:T(8,128)S(1)} %analyse.6), channel_id=1, source_target_pairs={{0,8},{8,0},{16,24},{24,16},{1,9},{9,1},{17,25},{25,17},{2,10},{10... | collective-permute-start | bytes 1229768 | tf_op jit(solution)/shard_map/ppermute | solution.py:632
  94.1 20.7 %copy-start.2 = (f32[2]{0:T(128)S(1)}, f32[2]{0:T(128)}, u32[]{:S(2)}) copy-start(f32[2]{0:T(128)} %damping_ref.7) | copy-start | bytes 28
  104.9 21.2 %collective-permute-start.4 = (f32[10,8,1281]{2,1,0:T(8,128)S(1)}, f32[10,8,1281]{2,1,0:T(8,128)S(1)}, u32[]{:S(2)}, u32[]{:S(2)}) collective-permute-start(f32[10,8,1281]{2,1,0:T(8,128)S(1)} %add.28.spectrum_ref), channel_id=1, source_target_pairs={{0,8},{8,0},{16,24},{24,16},{1,9},{9,1},{17,25},{25,17},{2,10},{10... | collective-permute-start | bytes 1229768 | tf_op jit(solution)/shard_map/ppermute | solution.py:632
  113.7 27.6 %collective-permute-start.6 = (f32[10,8,1281]{2,1,0:T(8,128)S(1)}, f32[10,8,1281]{2,1,0:T(8,128)S(1)}, u32[]{:S(2)}, u32[]{:S(2)}) collective-permute-start(f32[10,8,1281]{2,1,0:T(8,128)S(1)} %add.29), channel_id=1, source_target_pairs={{0,16},{8,24},{16,0},{24,8},{1,17},{9,25},{17,1},{25,9},{2,18},{10... | collective-permute-start | bytes 1229768 | tf_op jit(solution)/shard_map/ppermute | solution.py:632
  137.5 30.4 %all-to-all-start.3 = ((f32[8,160,128]{2,1,0:T(8,128)}), f32[8,160,128]{2,1,0:T(8,128)S(1)}, u32[]{:S(2)}, u32[]{:S(2)}) async-start(f32[8,160,128]{2,1,0:T(8,128)} %synthesise.5), calls=%async_computation.3 | async-start | bytes 1310720 | tf_op jit(solution)/shard_map/all_to_all | solution.py:611
  141.4 15.8 %collective-permute-start.7 = (f32[10,8,1281]{2,1,0:T(8,128)S(1)}, f32[10,8,1281]{2,1,0:T(8,128)S(1)}, u32[]{:S(2)}, u32[]{:S(2)}) collective-permute-start(f32[10,8,1281]{2,1,0:T(8,128)S(1)} %add.30.spectrum_ref), channel_id=1, source_target_pairs={{0,8},{8,0},{16,24},{24,16},{1,9},{9,1},{17,25},{25,17},{2,10},{10... | collective-permute-start | bytes 1229768 | tf_op jit(solution)/shard_map/ppermute | solution.py:632
  156.8 25.8 %copy-start.1 = (f32[9,2,160,128]{3,2,1,0:T(8,128)S(1)}, f32[9,2,160,128]{3,2,1,0:T(8,128)}, u32[]{:S(2)}) copy-start(f32[9,2,160,128]{3,2,1,0:T(8,128)} %copy-done) | copy-start | bytes 4423684
  156.8 25.8 %copy-start.5 = (bf16[320,320]{1,0:T(8,128)(2,1)S(1)}, bf16[320,320]{1,0:T(8,128)(2,1)}, u32[]{:S(2)}) copy-start(bf16[320,320]{1,0:T(8,128)(2,1)} %constant.47.clone.refs_2_) | copy-start | bytes 614404
  156.8 25.8 %copy-start.6 = (bf16[320,320]{1,0:T(8,128)(2,1)S(1)}, bf16[320,320]{1,0:T(8,128)(2,1)}, u32[]{:S(2)}) copy-start(bf16[320,320]{1,0:T(8,128)(2,1)} %constant.48.clone.refs_3_) | copy-start | bytes 614404
